TPU v7x, 8 devices: a whole 2x2x1 slice. The times are simulated.
8 devices in a mesh: dp: 2 (over z, y), tp: 4 (over x, core).
Axes of the slice: x: 2, y: 2, z: 1, core: 2. Of those that a mesh axis runs over, the one named last changes fastest.
Arguments:
- x_in: bfloat16 [256, 4096], P('dp'), parts along dimension 0
- tok_pos: int32 [256], P('dp'), parts along dimension 0
- conv_state: bfloat16 [2, 256, 3, 5632], P(None, 'dp', None, 'tp'), parts along dimension 1
- lru_state: float32 [2, 256, 5632], P(None, 'dp', 'tp'), parts along dimension 1
- k_cache: bfloat16 [256, 1024, 128], P('dp'), parts along dimension 0
- v_cache: bfloat16 [256, 1024, 128], P('dp'), parts along dimension 0
- slot_pos: int32 [256, 1024], P('dp'), parts along dimension 0
- norm_scale: bfloat16 [3, 2, 4096], replicated
- rec_wx: bfloat16 [2, 4096, 5632], P(None, None, 'tp')
- rec_bx: bfloat16 [2, 5632], P(None, 'tp')
- rec_wy: bfloat16 [2, 4096, 5632], P(None, None, 'tp')
- rec_by: bfloat16 [2, 5632], P(None, 'tp')
- conv_w: bfloat16 [2, 4, 5632], P(None, None, 'tp')
- conv_b: bfloat16 [2, 5632], P(None, 'tp')
- gate_wa: bfloat16 [2, 32, 176, 176], P(None, 'tp')
- gate_ba: bfloat16 [2, 5632], P(None, 'tp')
- gate_wi: bfloat16 [2, 32, 176, 176], P(None, 'tp')
- gate_bi: bfloat16 [2, 5632], P(None, 'tp')
- a_param: float32 [2, 5632], P(None, 'tp')
- rec_wout: bfloat16 [2, 5632, 4096], P(None, 'tp')
- rec_bout: bfloat16 [2, 4096], replicated
- attn_wq: bfloat16 [4096, 4096], P(None, 'tp')
- attn_wk: bfloat16 [4096, 128], replicated
- attn_wv: bfloat16 [4096, 128], replicated
- attn_wo: bfloat16 [4096, 4096], P('tp')
- attn_bo: bfloat16 [4096], replicated
- mlp_w1: bfloat16 [3, 4096, 12288], P(None, None, 'tp')
- mlp_b1: bfloat16 [3, 12288], P(None, 'tp')
- mlp_w2: bfloat16 [3, 4096, 12288], P(None, None, 'tp')
- mlp_b2: bfloat16 [3, 12288], P(None, 'tp')
- mlp_wd: bfloat16 [3, 12288, 4096], P(None, 'tp')
- mlp_bd: bfloat16 [3, 4096], replicated
Outputs:
- output 1: bfloat16 [256, 4096], P('dp'), parts along dimension 0
- output 2: bfloat16 [2, 256, 3, 5632], P(None, 'dp', None, 'tp'), parts along dimension 1
- output 3: float32 [2, 256, 5632], P(None, 'dp', 'tp'), parts along dimension 1
- output 4: bfloat16 [256, 1024, 128], P('dp'), parts along dimension 0
- output 5: bfloat16 [256, 1024, 128], P('dp'), parts along dimension 0
- output 6: int32 [256, 1024], P('dp'), parts along dimension 0
There are 2 independent parts. A program takes and returns all parts, laid end to end along the dimension named above; an argument that names none is the same for every part.
All inputs are finite; a program needn't handle non-finite values.
Results may differ from a plain program's by a relative error of at most 0.02.
Values are sent between devices in bfloat16 or wider.
A program may use at most 1.75 GiB of HBM per device.

v0:
```python
import jax
import jax.numpy as jnp
from jax import lax
from jax.sharding import PartitionSpec as P

ROPE_BASE = 10000.0
NORM_EPS = 1e-6


def rms_norm(residual, scale):
    res_f = residual.astype(jnp.float32)
    mean_sq = jnp.mean(res_f * res_f, axis=-1, keepdims=True)
    return (res_f * lax.rsqrt(mean_sq + NORM_EPS) * (1.0 + scale.astype(jnp.float32))).astype(jnp.bfloat16)


def add_update(residual, update, out_bias):
    return (residual.astype(jnp.float32) + update.astype(jnp.bfloat16).astype(jnp.float32) + out_bias.astype(jnp.float32)).astype(jnp.bfloat16)


def rope_tables(tok_pos, head_dim):
    quarter = head_dim // 4
    inv_freq = ROPE_BASE ** (-jnp.arange(quarter, dtype=jnp.float32) / quarter)
    angles = tok_pos.astype(jnp.float32)[:, None] * inv_freq[None, :]
    return jnp.cos(angles), jnp.sin(angles)


def apply_rope(vectors, cosine, sine):
    quarter = vectors.shape[-1] // 4
    first = vectors[..., :quarter]
    second = vectors[..., quarter:2 * quarter]
    return jnp.concatenate([first * cosine - second * sine, second * cosine + first * sine, vectors[..., 2 * quarter:]], axis=-1)


def mlp_update(normed, w_up, b_up, w_lin, b_lin, w_down):
    gate_pre = jnp.dot(normed, w_up, preferred_element_type=jnp.float32) + b_up.astype(jnp.float32)
    lin_pre = jnp.dot(normed, w_lin, preferred_element_type=jnp.float32) + b_lin.astype(jnp.float32)
    hidden = (jax.nn.gelu(gate_pre, approximate=True) * lin_pre).astype(jnp.bfloat16)
    return jnp.dot(hidden, w_down, preferred_element_type=jnp.float32)


def recurrent_update(normed, tok_pos, conv_prev, lru_prev, rec_wx, rec_bx, rec_wy, rec_by, conv_w, conv_b, gate_wa, gate_ba, gate_wi, gate_bi, a_param, rec_wout):
    n_rows = normed.shape[0]
    n_blocks = gate_wa.shape[0]
    block_width = gate_wa.shape[1]
    x_branch = (jnp.dot(normed, rec_wx, preferred_element_type=jnp.float32) + rec_bx.astype(jnp.float32)).astype(jnp.bfloat16)
    y_branch = jax.nn.gelu(jnp.dot(normed, rec_wy, preferred_element_type=jnp.float32) + rec_by.astype(jnp.float32), approximate=True)
    tap_keep = tok_pos[:, None, None] >= jnp.arange(3, 0, -1, dtype=jnp.int32)[None, :, None]
    history = jnp.where(tap_keep, conv_prev.astype(jnp.float32), 0.0)
    tap_w = conv_w.astype(jnp.float32)
    conv_sum = conv_b.astype(jnp.float32) + tap_w[0] * x_branch.astype(jnp.float32) + jnp.sum(history * tap_w[:0:-1][None], axis=1)
    conv_x = conv_sum.astype(jnp.bfloat16)
    blocks = conv_x.reshape(n_rows, n_blocks, block_width)
    r_pre = jnp.einsum('bhi,hij->bhj', blocks, gate_wa, preferred_element_type=jnp.float32).reshape(n_rows, -1) + gate_ba.astype(jnp.float32)
    i_pre = jnp.einsum('bhi,hij->bhj', blocks, gate_wi, preferred_element_type=jnp.float32).reshape(n_rows, -1) + gate_bi.astype(jnp.float32)
    log_a = -8.0 * jax.nn.sigmoid(r_pre) * jax.nn.softplus(a_param)
    decay_gate = jnp.exp(log_a)
    in_scale = jnp.sqrt(1.0 - decay_gate * decay_gate)
    is_reset = (tok_pos == 0)[:, None]
    decay_gate = jnp.where(is_reset, 0.0, decay_gate)
    in_scale = jnp.where(is_reset, 1.0, in_scale)
    lru_new = decay_gate * lru_prev + in_scale * jax.nn.sigmoid(i_pre) * conv_x.astype(jnp.float32)
    gated_h = (lru_new * y_branch).astype(jnp.bfloat16)
    update = jnp.dot(gated_h, rec_wout, preferred_element_type=jnp.float32)
    conv_new = jnp.concatenate([conv_prev[:, 1:], x_branch[:, None, :]], axis=1)
    return update, conv_new, lru_new


def project_qkv(normed, tok_pos, attn_wq, attn_wk, attn_wv):
    n_rows = normed.shape[0]
    head_dim = attn_wk.shape[1]
    cosine, sine = rope_tables(tok_pos, head_dim)
    q_heads = jnp.dot(normed, attn_wq, preferred_element_type=jnp.float32).reshape(n_rows, -1, head_dim)
    q_heads = apply_rope(q_heads, cosine[:, None, :], sine[:, None, :]).astype(jnp.bfloat16)
    k_new = apply_rope(jnp.dot(normed, attn_wk, preferred_element_type=jnp.float32), cosine, sine).astype(jnp.bfloat16)
    v_new = jnp.dot(normed, attn_wv, preferred_element_type=jnp.float32).astype(jnp.bfloat16)
    return q_heads, k_new, v_new


def write_cache(tok_pos, k_new, v_new, k_cache, v_cache, slot_pos):
    window = k_cache.shape[1]
    target = jnp.arange(window, dtype=jnp.int32)[None, :] == (tok_pos % window)[:, None]
    k_next = jnp.where(target[:, :, None], k_new[:, None, :], k_cache)
    v_next = jnp.where(target[:, :, None], v_new[:, None, :], v_cache)
    slot_next = jnp.where(target, tok_pos[:, None], slot_pos)
    return k_next, v_next, slot_next


def attend(q_heads, tok_pos, k_next, v_next, slot_next, attn_wo):
    n_rows = q_heads.shape[0]
    window = k_next.shape[1]
    head_dim = k_next.shape[2]
    slot_age = tok_pos[:, None] - slot_next
    slot_valid = (slot_next >= 0) & (slot_age >= 0) & (slot_age < window)
    scores = jnp.einsum('bhd,bsd->bhs', q_heads, k_next, preferred_element_type=jnp.float32) * (head_dim ** -0.5)
    scores = jnp.where(slot_valid[:, None, :], scores, -jnp.inf)
    probs_bf = jax.nn.softmax(scores, axis=-1).astype(jnp.bfloat16)
    heads_out = jnp.einsum('bhs,bsd->bhd', probs_bf, v_next, preferred_element_type=jnp.float32).astype(jnp.bfloat16)
    return jnp.dot(heads_out.reshape(n_rows, -1), attn_wo, preferred_element_type=jnp.float32)


def io_specs():
    in_specs = (P('dp', None), P('dp'), P(None, 'dp', None, 'tp'), P(None, 'dp', 'tp'), P('dp', None, None), P('dp', None, None), P('dp', None),
                P(), P(None, None, 'tp'), P(None, 'tp'), P(None, None, 'tp'), P(None, 'tp'), P(None, None, 'tp'), P(None, 'tp'),
                P(None, 'tp', None, None), P(None, 'tp'), P(None, 'tp', None, None), P(None, 'tp'), P(None, 'tp'), P(None, 'tp', None), P(),
                P(None, 'tp'), P(), P(), P('tp', None), P(),
                P(None, None, 'tp'), P(None, 'tp'), P(None, None, 'tp'), P(None, 'tp'), P(None, 'tp', None), P())
    out_specs = (P('dp', None), P(None, 'dp', None, 'tp'), P(None, 'dp', 'tp'), P('dp', None, None), P('dp', None, None), P('dp', None))
    return in_specs, out_specs


def solution(mesh):
    in_specs, out_specs = io_specs()

    def local_step(x_in, tok_pos, conv_state, lru_state, k_cache, v_cache, slot_pos, norm_scale, rec_wx, rec_bx, rec_wy, rec_by, conv_w, conv_b, gate_wa, gate_ba, gate_wi, gate_bi, a_param, rec_wout, rec_bout, attn_wq, attn_wk, attn_wv, attn_wo, attn_bo, mlp_w1, mlp_b1, mlp_w2, mlp_b2, mlp_wd, mlp_bd):
        residual = x_in
        conv_list = []
        lru_list = []
        for layer_idx in range(3):
            normed = rms_norm(residual, norm_scale[layer_idx, 0])
            if layer_idx < 2:
                part_sum, conv_new, lru_new = recurrent_update(normed, tok_pos, conv_state[layer_idx], lru_state[layer_idx], rec_wx[layer_idx], rec_bx[layer_idx], rec_wy[layer_idx], rec_by[layer_idx], conv_w[layer_idx], conv_b[layer_idx], gate_wa[layer_idx], gate_ba[layer_idx], gate_wi[layer_idx], gate_bi[layer_idx], a_param[layer_idx], rec_wout[layer_idx])
                conv_list.append(conv_new)
                lru_list.append(lru_new)
                out_bias = rec_bout[layer_idx]
            else:
                q_heads, k_new, v_new = project_qkv(normed, tok_pos, attn_wq, attn_wk, attn_wv)
                k_next, v_next, slot_next = write_cache(tok_pos, k_new, v_new, k_cache, v_cache, slot_pos)
                part_sum = attend(q_heads, tok_pos, k_next, v_next, slot_next, attn_wo)
                out_bias = attn_bo
            residual = add_update(residual, lax.psum(part_sum.astype(jnp.bfloat16), 'tp'), out_bias)
            normed = rms_norm(residual, norm_scale[layer_idx, 1])
            part_sum = mlp_update(normed, mlp_w1[layer_idx], mlp_b1[layer_idx], mlp_w2[layer_idx], mlp_b2[layer_idx], mlp_wd[layer_idx])
            residual = add_update(residual, lax.psum(part_sum.astype(jnp.bfloat16), 'tp'), mlp_bd[layer_idx])
        return (residual, jnp.stack(conv_list), jnp.stack(lru_list), k_next, v_next, slot_next)

    return jax.shard_map(local_step, mesh=mesh, in_specs=in_specs, out_specs=out_specs, check_vma=False)
```

profile of v0, /device:TPU:0, one launch (start us, length us, event | category | flops | bytes accessed | tf_op | source)
XLA Modules:
  0.0 468.8 jit_solution(3030115379311929229)
XLA Ops:
  9.3 1.2 broadcast_compare_fusion.1
  11.2 1.5 convert_add_fusion.6
  12.7 1.5 fusion.122
  14.2 1.5 convert_reduce_fusion.3
  15.7 3.3 multiply_reduce_fusion
  19.0 6.9 %add_convert_fusion.1 = (bf16[128,1408]{1,0:T(8,128)(2,1)S(1)}, bf16[128,1408]{1,0:T(8,128)(2,1)}) fusion(f32[128,1408]{1,0:T(8,128)S(1)} %get-tuple-element.7, f32[1408]{0:T(1024)S(1)} %slice_reduce_fusion.1, f32[1408]{0:T(1024)S(1)} %get-tuple-element.74, f32[1408]{0:T(1024)S(1)} %get-tuple-element.19, bf16[2,4096,1408]{2,1,0:T(8,128)(2,1)} %param.40, ...), kind=kOutput, calls=%fused_computation.204 | convolution fusion | flops 1479753728 | bytes 14058496 | tf_op jit(solution)/shard_map/dot_general | solution.py:45
  26.2 1.6 fusion.224
  28.9 1.6 fusion.222
  30.4 1.1 copy.57
  31.5 1.5 fusion.271
  33.0 1.4 convert_reduce_fusion
  34.4 1.4 convert_reduce_fusion.1
  35.9 2.3 fusion.227
  38.2 12.5 %fusion.46 = bf16[128,4096]{1,0:T(8,128)(2,1)} fusion(bf16[2,1408,4096]{2,1,0:T(8,128)(2,1)} %param.51, f32[128,1408]{1,0:T(8,128)S(1)} %fusion.227, bf16[2,4096,1408]{2,1,0:T(8,128)(2,1)} %param.42, f32[1408]{0:T(1024)S(1)} %get-tuple-element.11, bf16[128,4096]{1,0:T(8,128)(2,1)S(1)} %copy-done.6, f32[4096]{0:T(1024)S(1)} %bitcast.249, f32[128]{0:T(128)S(1)} %copy-done.42), kind=kOutput, calls=%fused_computation.48 | convolution fusion | flops 2957393920 | bytes 25909248 | tf_op jit(solution)/shard_map/dot_general | solution.py:63
  53.3 31.2 %all-reduce.7.cloned.1.call-done = bf16[128,4096]{1,0:T(8,128)(2,1)} async-done(((bf16[128,4096]{1,0:T(8,128)(2,1)}), bf16[128,4096]{1,0:T(8,128)(2,1)}) %all-reduce.7.cloned.1.call-update) | async-done | bytes 1048592 | tf_op jit(solution)/shard_map/psum | solution.py:130
  84.5 1.7 fusion.127
  86.2 11.4 %fusion.163 = f32[128,3072]{1,0:T(8,128)} fusion(bf16[3,4096,3072]{2,1,0:T(8,128)(2,1)} %param.58, f32[3072]{0:T(1024)S(1)} %bitcast.254, bf16[128,4096]{1,0:T(8,128)(2,1)S(1)} %get-tuple-element.31, f32[4096]{0:T(1024)S(1)} %bitcast.246, f32[128]{0:T(128)S(1)} %add_rsqrt_fusion.4), kind=kOutput, calls=%fused_computation.141 | convolution fusion | flops 3226861568 | bytes 27816448 | tf_op jit(solution)/shard_map/dot_general | solution.py:35
  97.7 19.6 %fusion.52 = bf16[128,4096]{1,0:T(8,128)(2,1)} fusion(bf16[3,3072,4096]{2,1,0:T(8,128)(2,1)} %param.62, f32[128,3072]{1,0:T(8,128)} %fusion.163, bf16[3,4096,3072]{2,1,0:T(8,128)(2,1)} %param.60, f32[3072]{0:T(1024)S(1)} %bitcast.255, bf16[128,4096]{1,0:T(8,128)(2,1)S(1)} %get-tuple-element.31, f32[4096]{0:T(1024)S(1)} %bitcast.247, f32[128]{0:T(128)S(1)} %add_rsqrt_fusion.4), kind=kOutput, calls=%fused_computation.51 | convolution fusion | flops 6446252032 | bytes 54030848 | tf_op jit(solution)/shard_map/dot_general | solution.py:38
  118.2 30.4 %all-reduce.9.cloned.1.call-done = bf16[128,4096]{1,0:T(8,128)(2,1)} async-done(((bf16[128,4096]{1,0:T(8,128)(2,1)}), bf16[128,4096]{1,0:T(8,128)(2,1)}) %all-reduce.9.cloned.1.call-update) | async-done | bytes 1048592 | tf_op jit(solution)/shard_map/psum | solution.py:133
  148.6 1.7 fusion.132
  150.4 7.3 %add_convert_fusion = (bf16[128,1408]{1,0:T(8,128)(2,1)S(1)}, bf16[128,1408]{1,0:T(8,128)(2,1)}) fusion(f32[128,1408]{1,0:T(8,128)S(1)} %copy-done.15, f32[1408]{0:T(1024)S(1)} %slice_reduce_fusion, f32[1408]{0:T(1024)S(1)} %copy-done.37, f32[1408]{0:T(1024)S(1)} %copy-done.36, bf16[2,4096,1408]{2,1,0:T(8,128)(2,1)} %param.40, ...), kind=kOutput, calls=%fused_computation.201 | convolution fusion | flops 1479753728 | bytes 14058496 | tf_op jit(solution)/shard_map/dot_general | solution.py:45
  157.9 1.6 fusion.220
  159.5 1.6 fusion.218
  162.5 2.9 fusion.226
  165.4 12.9 %fusion.49 = bf16[128,4096]{1,0:T(8,128)(2,1)} fusion(bf16[2,1408,4096]{2,1,0:T(8,128)(2,1)} %param.51, f32[128,1408]{1,0:T(8,128)} %fusion.226, bf16[2,4096,1408]{2,1,0:T(8,128)(2,1)} %param.42, f32[1408]{0:T(1024)S(1)} %copy-done.38, bf16[128,4096]{1,0:T(8,128)(2,1)} %copy-done.7, f32[4096]{0:T(1024)S(1)} %bitcast.245, f32[128]{0:T(128)S(1)} %add_rsqrt_fusion.3), kind=kOutput, calls=%fused_computation.49 | convolution fusion | flops 2957393920 | bytes 25909248 | tf_op jit(solution)/shard_map/dot_general | solution.py:63
  178.6 1.5 slice_bitcast_fusion.1
  180.1 29.5 %all-reduce.11.cloned.1.call-done = bf16[128,4096]{1,0:T(8,128)(2,1)} async-done(((bf16[128,4096]{1,0:T(8,128)(2,1)}), bf16[128,4096]{1,0:T(8,128)(2,1)}) %all-reduce.11.cloned.1.call-update) | async-done | bytes 1048592 | tf_op jit(solution)/shard_map/psum | solution.py:130
  209.6 2.1 fusion.137
  211.7 11.8 %fusion.172 = f32[128,3072]{1,0:T(8,128)} fusion(bf16[3,4096,3072]{2,1,0:T(8,128)(2,1)} %param.58, f32[3072]{0:T(1024)S(1)} %bitcast.252, bf16[128,4096]{1,0:T(8,128)(2,1)S(1)} %get-tuple-element.27, f32[4096]{0:T(1024)S(1)} %bitcast.242, f32[128]{0:T(128)S(1)} %add_rsqrt_fusion.2), kind=kOutput, calls=%fused_computation.148 | convolution fusion | flops 3226861568 | bytes 27816448 | tf_op jit(solution)/shard_map/dot_general | solution.py:35
  223.5 19.7 %fusion.55 = bf16[128,4096]{1,0:T(8,128)(2,1)} fusion(bf16[3,3072,4096]{2,1,0:T(8,128)(2,1)} %param.62, f32[128,3072]{1,0:T(8,128)} %fusion.172, bf16[3,4096,3072]{2,1,0:T(8,128)(2,1)} %param.60, f32[3072]{0:T(1024)S(1)} %bitcast.253, bf16[128,4096]{1,0:T(8,128)(2,1)S(1)} %get-tuple-element.27, f32[4096]{0:T(1024)S(1)} %bitcast.243, f32[128]{0:T(128)S(1)} %add_rsqrt_fusion.2), kind=kOutput, calls=%fused_computation.52 | convolution fusion | flops 6446252032 | bytes 54030848 | tf_op jit(solution)/shard_map/dot_general | solution.py:38
  246.6 27.9 %all-reduce.13.cloned.1.call-done = bf16[128,4096]{1,0:T(8,128)(2,1)} async-done(((bf16[128,4096]{1,0:T(8,128)(2,1)}), bf16[128,4096]{1,0:T(8,128)(2,1)}) %all-reduce.13.cloned.1.call-update) | async-done | bytes 1048592 | tf_op jit(solution)/shard_map/psum | solution.py:133
  274.5 2.1 fusion.142
  276.5 4.7 %convolution_bitcast_fusion = f32[16,8,8,128]{3,1,2,0:T(8,128)S(1)} fusion(bf16[4096,1024]{1,0:T(8,128)(2,1)} %param.53, bf16[128,4096]{1,0:T(8,128)(2,1)S(1)} %get-tuple-element.25, f32[4096]{0:T(1024)S(1)} %bitcast.232, f32[128]{0:T(128)S(1)} %add_rsqrt_fusion.1), kind=kOutput, calls=%fused_computation.157 | convolution fusion | flops 1075838976 | bytes 9978368 | tf_op jit(solution)/shard_map/dot_general | solution.py:72
  282.4 1.7 convolution_convert_fusion.1
  284.7 44.3 %broadcast_select_fusion.1 = (bf16[128,1024,128]{2,1,0:T(8,128)(2,1)}, bf16[128,1024,128]{2,1,0:T(8,128)(2,1)}) fusion(bf16[128,1024,128]{2,1,0:T(8,128)(2,1)} %param.36, pred[128,1024]{1,0:T(8,128)(4,1)S(1)} %get-tuple-element.63, bf16[128,128]{1,0:T(8,128)(2,1)S(1)} %copy.65, bf16[128,1024,128]{2,1,0:T(8,128)(2,1)} %param.37, ...), kind=kLoop, calls=%fused_computation.2 | loop fusion | flops 33554432 | bytes 134414336 | tf_op jit(solution)/shard_map/jit(_where)/select_n | solution.py:82
  329.0 14.0 %fusion.263 = f32[128,8,1024]{2,1,0:T(8,128)S(1)} fusion(bf16[128,1024,128]{2,1,0:T(8,128)(2,1)} %get-tuple-element.36, bf16[128,8,64]{2,1,0:T(8,128)(2,1)S(1)} %slice.491, bf16[128,8,32]{2,1,0:T(8,128)(2,1)S(1)} %get-tuple-element.35, bf16[128,8,32]{2,1,0:T(8,128)(2,1)S(1)} %get-tuple-element.34), kind=kOutput, calls=%fused_computation.222 | convolution fusion | flops 269221888 | bytes 38010880 | tf_op jit(solution)/shard_map/bhd,bsd->bhs/dot_general | solution.py:94
  343.1 3.4 fusion.295
  346.5 14.3 %fusion.184 = bf16[128,8,128]{2,1,0:T(8,128)(2,1)S(1)} fusion(bf16[128,1024,128]{2,1,0:T(8,128)(2,1)} %get-tuple-element.37, f32[128,8,1024]{2,1,0:T(8,128)} %get-tuple-element.71, f32[128,8]{1,0:T(8,128)S(1)} %get-tuple-element.70), kind=kOutput, calls=%fused_computation.158 | convolution fusion | flops 270663680 | bytes 38014976 | tf_op jit(solution)/shard_map/bhs,bsd->bhd/dot_general | solution.py:97
  360.8 2.3 convolution_convert_fusion
  363.5 2.1 maximum_bitcast_fusion
  365.5 2.3 pad_maximum_fusion.1
  367.8 26.5 %all-reduce.15.cloned.1.call-done = bf16[128,4096]{1,0:T(8,128)(2,1)} async-done(((bf16[128,4096]{1,0:T(8,128)(2,1)}), bf16[128,4096]{1,0:T(8,128)(2,1)}) %all-reduce.15.cloned.1.call-update) | async-done | bytes 1048592 | tf_op jit(solution)/shard_map/psum | solution.py:130
  394.4 1.7 fusion.147
  396.2 11.8 %fusion.181 = f32[128,3072]{1,0:T(8,128)} fusion(bf16[3,4096,3072]{2,1,0:T(8,128)(2,1)} %param.58, f32[3072]{0:T(1024)S(1)} %bitcast.250, bf16[128,4096]{1,0:T(8,128)(2,1)S(1)} %get-tuple-element.21, f32[4096]{0:T(1024)S(1)} %bitcast.240, f32[128]{0:T(128)S(1)} %add_rsqrt_fusion), kind=kOutput, calls=%fused_computation.155 | convolution fusion | flops 3226861568 | bytes 27816448 | tf_op jit(solution)/shard_map/dot_general | solution.py:35
  408.0 19.7 %fusion.58 = bf16[128,4096]{1,0:T(8,128)(2,1)} fusion(bf16[3,3072,4096]{2,1,0:T(8,128)(2,1)} %param.62, f32[128,3072]{1,0:T(8,128)} %fusion.181, bf16[3,4096,3072]{2,1,0:T(8,128)(2,1)} %param.60, f32[3072]{0:T(1024)S(1)} %bitcast.251, bf16[128,4096]{1,0:T(8,128)(2,1)S(1)} %get-tuple-element.21, f32[4096]{0:T(1024)S(1)} %bitcast.241, f32[128]{0:T(128)S(1)} %add_rsqrt_fusion), kind=kOutput, calls=%fused_computation.53 | convolution fusion | flops 6446252032 | bytes 54030848 | tf_op jit(solution)/shard_map/dot_general | solution.py:38
  428.9 1.6 pad_maximum_fusion
  430.5 28.5 %all-reduce.17.cloned.1.call-done = bf16[128,4096]{1,0:T(8,128)(2,1)} async-done(((bf16[128,4096]{1,0:T(8,128)(2,1)}), bf16[128,4096]{1,0:T(8,128)(2,1)}) %all-reduce.17.cloned.1.call-update) | async-done | bytes 1048592 | tf_op jit(solution)/shard_map/psum | solution.py:133
  458.9 2.5 fusion.151
  (143 shorter events, 16.2 us)
Async XLA Ops:
  7.2 274.2 %copy-start = (bf16[4096,128]{1,0:T(8,128)(2,1)S(1)}, bf16[4096,128]{1,0:T(8,128)(2,1)}, u32[]{:S(2)}) copy-start(bf16[4096,128]{1,0:T(8,128)(2,1)} %param.54) | copy-start | bytes 3145732
  7.2 77.3 %all-reduce.7.cloned.1.call-start = ((), (), s32[]{:S(2)}) async-start(), calls=%async_computation | async-start | bytes 2097152 | tf_op jit(solution)/shard_map/psum | solution.py:130
  12.7 6.3 %copy-start.31 = (f32[1,1,4096]{2,1,0:T(1,128)}, f32[1,1,4096]{2,1,0:T(1,128)S(1)}, u32[]{:S(2)}) copy-start(f32[1,1,4096]{2,1,0:T(1,128)S(1)} %get-tuple-element.44) | copy-start | bytes 49156
  14.2 4.8 %copy-start.6 = (bf16[128,4096]{1,0:T(8,128)(2,1)S(1)}, bf16[128,4096]{1,0:T(8,128)(2,1)}, u32[]{:S(2)}) copy-start(bf16[128,4096]{1,0:T(8,128)(2,1)} %param.32) | copy-start | bytes 3145732
  14.2 11.7 %copy-start.41 = (f32[128]{0:T(128)}, f32[128]{0:T(128)S(1)}, u32[]{:S(2)}) copy-start(f32[128]{0:T(128)S(1)} %add_rsqrt_fusion.5) | copy-start | bytes 1540
  31.5 6.6 %copy-start.32 = (f32[1,1,4096]{2,1,0:T(1,128)S(1)}, f32[1,1,4096]{2,1,0:T(1,128)}, u32[]{:S(2)}) copy-start(f32[1,1,4096]{2,1,0:T(1,128)} %copy-done.31) | copy-start | bytes 49156
  31.5 6.6 %copy-start.42 = (f32[128]{0:T(128)S(1)}, f32[128]{0:T(128)}, u32[]{:S(2)}) copy-start(f32[128]{0:T(128)} %copy-done.41) | copy-start | bytes 1540
  38.1 12.5 %copy-start.13 = (f32[128,1408]{1,0:T(8,128)}, f32[128,1408]{1,0:T(8,128)S(1)}, u32[]{:S(2)}) copy-start(f32[128,1408]{1,0:T(8,128)S(1)} %fusion.227) | copy-start | bytes 2162692
  38.1 13.9 %copy-start.21 = (bf16[2,4096]{1,0:T(2,128)(2,1)S(1)}, bf16[2,4096]{1,0:T(2,128)(2,1)}, u32[]{:S(2)}) copy-start(bf16[2,4096]{1,0:T(2,128)(2,1)} %param.52) | copy-start | bytes 49156
  38.2 13.9 %copy-start.22 = (bf16[3,3072]{1,0:T(4,128)(2,1)S(1)}, bf16[3,3072]{1,0:T(4,128)(2,1)}, u32[]{:S(2)}) copy-start(bf16[3,3072]{1,0:T(4,128)(2,1)} %param.59) | copy-start | bytes 55300
  38.2 14.5 %copy-start.23 = (bf16[3,3072]{1,0:T(4,128)(2,1)S(1)}, bf16[3,3072]{1,0:T(4,128)(2,1)}, u32[]{:S(2)}) copy-start(bf16[3,3072]{1,0:T(4,128)(2,1)} %param.61) | copy-start | bytes 55300
  50.6 35.6 %copy-start.30 = (f32[1,1,4096]{2,1,0:T(1,128)S(1)}, f32[1,1,4096]{2,1,0:T(1,128)}, u32[]{:S(2)}) copy-start(f32[1,1,4096]{2,1,0:T(1,128)} %get-tuple-element.43) | copy-start | bytes 49156
  50.7 97.9 %all-reduce.9.cloned.1.call-start = ((), (), s32[]{:S(2)}) async-start(), calls=%async_computation.1 | async-start | bytes 2097152 | tf_op jit(solution)/shard_map/psum | solution.py:133
  97.7 19.9 %copy-start.19 = (bf16[3,4096]{1,0:T(4,128)(2,1)S(1)}, bf16[3,4096]{1,0:T(4,128)(2,1)}, u32[]{:S(2)}) copy-start(bf16[3,4096]{1,0:T(4,128)(2,1)} %param.63) | copy-start | bytes 73732
  117.3 33.1 %copy-start.15 = (f32[128,1408]{1,0:T(8,128)S(1)}, f32[128,1408]{1,0:T(8,128)}, u32[]{:S(2)}) copy-start(f32[128,1408]{1,0:T(8,128)} %get-tuple-element.6) | copy-start | bytes 2162692
  117.3 33.1 %copy-start.29 = (f32[1,1,4096]{2,1,0:T(1,128)S(1)}, f32[1,1,4096]{2,1,0:T(1,128)}, u32[]{:S(2)}) copy-start(f32[1,1,4096]{2,1,0:T(1,128)} %get-tuple-element.42) | copy-start | bytes 49156
  117.3 33.1 %copy-start.36 = (f32[1408]{0:T(1024)S(1)}, f32[1408]{0:T(1024)}, u32[]{:S(2)}) copy-start(f32[1408]{0:T(1024)} %get-tuple-element.18) | copy-start | bytes 16900
  117.3 33.1 %copy-start.37 = (f32[1408]{0:T(1024)S(1)}, f32[1408]{0:T(1024)}, u32[]{:S(2)}) copy-start(f32[1408]{0:T(1024)} %get-tuple-element.75) | copy-start | bytes 16900
  117.3 92.3 %all-reduce.11.cloned.1.call-start = ((), (), s32[]{:S(2)}) async-start(), calls=%async_computation.2 | async-start | bytes 2097152 | tf_op jit(solution)/shard_map/psum | solution.py:130
  150.3 7.4 %copy-start.7 = (bf16[128,4096]{1,0:T(8,128)(2,1)}, bf16[128,4096]{1,0:T(8,128)(2,1)S(1)}, u32[]{:S(2)}) copy-start(bf16[128,4096]{1,0:T(8,128)(2,1)S(1)} %get-tuple-element.29) | copy-start | bytes 3145732
  159.5 3.0 copy-start.24
  159.5 3.0 copy-start.25
  159.5 3.0 copy-start.26
  159.5 3.0 copy-start.39
  162.2 3.2 copy-start.38
  165.4 13.1 %copy-start.2 = (bf16[2,128,3,1408]{3,1,2,0:T(8,128)(2,1)S(1)}, bf16[2,128,3,1408]{3,1,2,0:T(8,128)(2,1)}, u32[]{:S(2)}) copy-start(bf16[2,128,3,1408]{3,1,2,0:T(8,128)(2,1)} %param.34) | copy-start | bytes 6488068
  178.3 96.1 %all-reduce.13.cloned.1.call-start = ((), (), s32[]{:S(2)}) async-start(), calls=%async_computation.3 | async-start | bytes 2097152 | tf_op jit(solution)/shard_map/psum | solution.py:133
  180.1 31.6 %copy-start.28 = (f32[1,1,4096]{2,1,0:T(1,128)S(1)}, f32[1,1,4096]{2,1,0:T(1,128)}, u32[]{:S(2)}) copy-start(f32[1,1,4096]{2,1,0:T(1,128)} %get-tuple-element.41) | copy-start | bytes 49156
  211.7 11.8 %copy-start.8 = (bf16[128,4096]{1,0:T(8,128)(2,1)}, bf16[128,4096]{1,0:T(8,128)(2,1)S(1)}, u32[]{:S(2)}) copy-start(bf16[128,4096]{1,0:T(8,128)(2,1)S(1)} %get-tuple-element.27) | copy-start | bytes 3145732
  223.5 20.1 %copy-start.35 = (bf16[4096]{0:T(1024)(128)(2,1)S(1)}, bf16[4096]{0:T(1024)(128)(2,1)}, u32[]{:S(2)}) copy-start(bf16[4096]{0:T(1024)(128)(2,1)} %param.57) | copy-start | bytes 24580
  223.5 20.1 %copy-start.10 = (bf16[128,3,1408]{2,0,1:T(8,128)(2,1)S(1)}, bf16[128,3,1408]{2,0,1:T(8,128)(2,1)}, u32[]{:S(2)}) copy-start(bf16[128,3,1408]{2,0,1:T(8,128)(2,1)} %get-tuple-element.33) | copy-start | bytes 3244036
  243.2 2.3 copy-start.40
  243.2 151.2 %all-reduce.15.cloned.1.call-start = ((), (), s32[]{:S(2)}) async-start(), calls=%async_computation.4 | async-start | bytes 2097152 | tf_op jit(solution)/shard_map/psum | solution.py:130
  243.5 1.9 copy-start.16
  343.1 17.7 %slice-start = ((s8[8388608]{0:T(1024)(128)(4,1)}), s8[4194304]{0:T(1024)(128)(4,1)S(1)}, s32[]{:S(2)}) async-start(s8[8388608]{0:T(1024)(128)(4,1)} %bitcast.215), calls=%async_computation.6 | async-start | bytes 8388608
  346.5 14.3 %slice-start.1 = ((s8[8388608]{0:T(1024)(128)(4,1)}), s8[4194304]{0:T(1024)(128)(4,1)S(1)}, s32[]{:S(2)}) async-start(s8[8388608]{0:T(1024)(128)(4,1)} %bitcast.215), calls=%async_computation.7 | async-start | bytes 8388608
  360.8 2.6 copy-start.12
  363.1 2.5 copy-start.14
  363.1 95.8 %all-reduce.17.cloned.1.call-start = ((), (), s32[]{:S(2)}) async-start(), calls=%async_computation.5 | async-start | bytes 2097152 | tf_op jit(solution)/shard_map/psum | solution.py:133
  367.8 28.3 %copy-start.27 = (f32[1,1,4096]{2,1,0:T(1,128)S(1)}, f32[1,1,4096]{2,1,0:T(1,128)}, u32[]{:S(2)}) copy-start(f32[1,1,4096]{2,1,0:T(1,128)} %get-tuple-element.40) | copy-start | bytes 49156
  367.8 28.3 %copy-start.33 = (f32[1,3072]{1,0:T(1,128)S(1)}, f32[1,3072]{1,0:T(1,128)}, u32[]{:S(2)}) copy-start(f32[1,3072]{1,0:T(1,128)} %get-tuple-element.52) | copy-start | bytes 36868
  396.1 11.8 %copy-start.4 = (bf16[128,4096]{1,0:T(8,128)(2,1)}, bf16[128,4096]{1,0:T(8,128)(2,1)S(1)}, u32[]{:S(2)}) copy-start(bf16[128,4096]{1,0:T(8,128)(2,1)S(1)} %get-tuple-element.21) | copy-start | bytes 3145732
  396.2 11.8 %copy-start.34 = (f32[1,3072]{1,0:T(1,128)S(1)}, f32[1,3072]{1,0:T(1,128)}, u32[]{:S(2)}) copy-start(f32[1,3072]{1,0:T(1,128)} %get-tuple-element.49) | copy-start | bytes 36868
  407.9 19.8 %copy-start.11 = (bf16[128,2,1408]{2,0,1:T(8,128)(2,1)S(1)}, bf16[128,2,1408]{2,0,1:T(8,128)(2,1)}, u32[]{:S(2)}) copy-start(bf16[128,2,1408]{2,0,1:T(8,128)(2,1)} %slice.287) | copy-start | bytes 2162692
  408.0 19.8 %copy-start.17 = (bf16[128,1408]{1,0:T(8,128)(2,1)S(1)}, bf16[128,1408]{1,0:T(8,128)(2,1)}, u32[]{:S(2)}) copy-start(bf16[128,1408]{1,0:T(8,128)(2,1)} %get-tuple-element.69) | copy-start | bytes 1081348
  428.9 30.0 %copy-start.5 = (bf16[128,4096]{1,0:T(8,128)(2,1)S(1)}, bf16[128,4096]{1,0:T(8,128)(2,1)}, u32[]{:S(2)}) copy-start(bf16[128,4096]{1,0:T(8,128)(2,1)} %copy-done.4) | copy-start | bytes 3145732
  428.9 30.0 %copy-start.20 = (f32[1,4096]{1,0:T(1,128)S(1)}, f32[1,4096]{1,0:T(1,128)}, u32[]{:S(2)}) copy-start(f32[1,4096]{1,0:T(1,128)} %get-tuple-element.46) | copy-start | bytes 49156
  428.9 32.5 %copy-start.1 = (bf16[4096,128]{1,0:T(8,128)(2,1)S(1)}, bf16[4096,128]{1,0:T(8,128)(2,1)}, u32[]{:S(2)}) copy-start(bf16[4096,128]{1,0:T(8,128)(2,1)} %param.54) | copy-start | bytes 3145732
  (3 other events, 3.2 us)
Sparse Core Ops, SparseCore 0:
  50.8 33.6 all-reduce.6
  117.4 31.0 all-reduce.8
  178.4 31.1 all-reduce.10
  243.3 31.0 all-reduce.12
  363.2 31.0 all-reduce.14
  427.8 31.0 all-reduce.16
where the time goes:
time: 477 us; the launch traced here: 469 us
  matrix products  177 us (37%)
  waiting for transfers between devices  174 us (36%)
  other arithmetic  89.2 us (19%)
  between operations  15.3 us (3%)
  local copies, waits for them, and re-layouts  11.3 us (2%)
    psum x6, waiting for transfers between devices, local_step(): lax.psum(part_sum.astype(jnp.bfloat16), 'tp')  174 us
    dot_general x3, matrix products, mlp_update(): return jnp.dot(hidden, w_down, preferred_element_type=jnp.float32)  59 us
    select_n x1, other arithmetic, write_cache(): k_next = jnp.where(target[:, :, None], k_new[:, None, :], k_cache)  44.3 us
    dot_general x3, matrix products, mlp_update(): jnp.dot(normed, w_up, preferred_element_type=jnp.float32)  35 us
    dot_general x2, matrix products, recurrent_update(): update = jnp.dot(gated_h, rec_wout, preferred_element_type=jnp.float32)  25.3 us
    dot_general x1, matrix products, attend(): jnp.einsum('bhs,bsd->bhd', probs_bf, v_next, preferred_element_type=jnp.f...  14.3 us
    dot_general x2, matrix products, recurrent_update(): jnp.dot(normed, rec_wx, preferred_element_type=jnp.float32)  14.2 us
    dot_general x1, matrix products, attend(): jnp.einsum('bhd,bsd->bhs', q_heads, k_next, preferred_element_type=jnp.fl...  14 us
  transfers between devices with their start and end apart: 6, of which 6 were waited for; matrix products, arithmetic and copies ran while one was open for 3% of the time, Pallas kernels for 0%

commit v1 on v0

v1 whole, which is shorter than its diff:
```python
import jax
import jax.numpy as jnp
from jax import lax
from jax.experimental import pallas as pl
from jax.experimental.pallas import tpu as pltpu
from jax.sharding import PartitionSpec as P

ROPE_BASE = 10000.0
NORM_EPS = 1e-6
BF = jnp.bfloat16
F32 = jnp.float32
ROWS = 128
D = 4096
TILE = 256
CHUNK = 512
N_CHUNK = D // CHUNK
HALF = ROWS // 2
VMEM_LIMIT = 67043328


class Stream:
    def __init__(self, slots, sems, n_slots):
        self.slots, self.sems, self.n_slots = slots, sems, n_slots
        self.phases = []
        self.total = 0

    def add(self, n, *kinds):
        start = self.total
        self.phases.append((start, n, kinds))
        self.total += n
        return start, kinds

    def slot_of(self, t):
        return lax.rem(t, self.n_slots)

    def copies(self, kind, j, slot):
        return [pltpu.make_async_copy(src, self.slots.at[(slot,) + dst], self.sems.at[slot, i]) for i, (src, dst) in enumerate(kind(j))]

    def start_tile(self, kinds, j, slot):
        n = len(kinds)
        if n == 1:
            for c in self.copies(kinds[0], j, slot):
                c.start()
            return
        for which, kind in enumerate(kinds):
            @pl.when(lax.rem(j, n) == which)
            def _(kind=kind):
                for c in self.copies(kind, lax.div(j, n), slot):
                    c.start()

    def issue(self, t, lo, hi):
        for start, n, kinds in self.phases:
            if start + n <= lo or hi <= start:
                continue

            def go(start=start, kinds=kinds):
                self.start_tile(kinds, t - start, self.slot_of(t))

            if start <= lo and hi <= start + n:
                go()
            else:
                pl.when(jnp.logical_and(t >= start, t < start + n))(go)

    def prime(self):
        first = min(self.n_slots, self.total)
        for start, n, kinds in self.phases:
            stop = min(start + n, first)
            if start < stop:
                @pl.loop(start, stop)
                def _(t, start=start, kinds=kinds):
                    self.start_tile(kinds, t - start, self.slot_of(t))

    def wait(self, phase, j):
        start, kinds = phase
        slot = self.slot_of(start + j)
        for c in self.copies(kinds[0], lax.div(j, len(kinds)), slot):
            c.wait()
        return slot


def full(slot_rows):
    return (pl.ds(0, slot_rows), pl.ds(0, TILE))


def columns(ref, layer, rows):
    return lambda j: [(ref.at[layer, :, pl.ds(pl.multiple_of(j * TILE, TILE), TILE)], full(rows))]


def gelu(v):
    return jax.nn.gelu(v, approximate=True)


def f32(v):
    return v.astype(F32)


def cols(k, width=CHUNK):
    return pl.ds(pl.multiple_of(k * width, width), width)


class Comm:
    def __init__(self, part, r1, cs, r2, fin, r3, s1, q1, s2, q2, s3, q3):
        self.part, self.r1, self.cs, self.r2, self.fin, self.r3 = part, r1, cs, r2, fin, r3
        self.s1, self.q1, self.s2, self.q2, self.s3, self.q3 = s1, q1, s2, q2, s3, q3
        me = lax.axis_index('tp')
        self.mine = lax.rem(me, 2)
        self.other = 1 - self.mine
        self.partner = me + 1 - 2 * self.mine
        self.peer = lax.rem(me + 2, 4)

    def barrier(self):
        sem = pltpu.get_barrier_semaphore()
        for dev in (self.partner, self.peer):
            pl.semaphore_signal(sem, inc=1, device_id={'tp': dev}, device_id_type=pl.DeviceIdType.MESH)
        pl.semaphore_wait(sem, 2)

    def copy1(self, par, k):
        return pltpu.make_async_remote_copy(src_ref=self.part.at[k, self.other], dst_ref=self.r1.at[k], send_sem=self.s1.at[par, k], recv_sem=self.q1.at[par, k], device_id={'tp': self.partner}, device_id_type=pl.DeviceIdType.MESH)

    def copy2(self, par, k):
        return pltpu.make_async_remote_copy(src_ref=self.cs.at[k], dst_ref=self.r2.at[par, k], send_sem=self.s2.at[par, k], recv_sem=self.q2.at[par, k], device_id={'tp': self.peer}, device_id_type=pl.DeviceIdType.MESH)

    def copy3(self, par, k):
        return pltpu.make_async_remote_copy(src_ref=self.fin.at[k], dst_ref=self.r3.at[k], send_sem=self.s3.at[par, k], recv_sem=self.q3.at[par, k], device_id={'tp': self.partner}, device_id_type=pl.DeviceIdType.MESH)

    def chip_sum(self, par, k):
        self.copy1(par, k).wait_recv()
        self.cs[k] = (f32(self.part[k, self.mine]) + f32(self.r1[k])).astype(BF)
        self.copy2(par, k).start()

    def finish(self, par, update):
        @pl.loop(0, N_CHUNK)
        def _(k):
            self.copy2(par, k).wait_recv()
            total = (f32(self.cs[k]) + f32(self.r2[par, k])).astype(BF)
            self.fin[k] = total
            self.copy3(par, k).start()
            update(self.mine, k, f32(total))

            @pl.when(k >= 1)
            def _():
                self.copy3(par, k - 1).wait_recv()
                update(self.other, k - 1, f32(self.r3[k - 1]))

        self.copy3(par, N_CHUNK - 1).wait_recv()
        update(self.other, N_CHUNK - 1, f32(self.r3[N_CHUNK - 1]))

        @pl.loop(0, N_CHUNK)
        def _(k):
            self.copy1(par, k).wait_send()
            self.copy2(par, k).wait_send()
            self.copy3(par, k).wait_send()


def fold_lanes(v):
    acc = v[:, 0:128]
    for i in range(1, v.shape[1] // 128):
        acc = acc + v[:, 128 * i:128 * (i + 1)]
    return acc


class Body:
    def __init__(self, stream, comm, x, n, hid, ss, nscale):
        self.stream, self.comm, self.x, self.n, self.hid, self.ss, self.nscale = stream, comm, x, n, hid, ss, nscale
        self.n_ar = 0

    def squares(self):
        self.ss[...] = jnp.zeros_like(self.ss)

        @pl.loop(0, N_CHUNK)
        def _(k):
            v = f32(self.x[:, cols(k)])
            self.ss[...] += fold_lanes(v * v)

    def norm(self, row):
        scale = lax.rsqrt(jnp.sum(self.ss[...], axis=-1, keepdims=True) * (1.0 / D) + NORM_EPS)

        @pl.loop(0, N_CHUNK)
        def _(k):
            gain = 1.0 + f32(self.nscale[row:row + 1, cols(k)])
            self.n[:, cols(k)] = (f32(self.x[:, cols(k)]) * scale * gain).astype(BF)

    def updater(self, bias, row):
        def update(half, k, u):
            rows = pl.ds(pl.multiple_of(half * HALF, HALF), HALF)
            new = (f32(self.x[rows, cols(k)]) + u + f32(bias[row:row + 1, cols(k)])).astype(BF)
            self.x[rows, cols(k)] = new
            v = f32(new)
            self.ss[rows, :] += fold_lanes(v * v)

        return update

    def all_reduce(self, bias, row):
        par = self.n_ar % 2
        self.n_ar += 1
        self.ss[...] = jnp.zeros_like(self.ss)
        self.comm.finish(par, self.updater(bias, row))

    def down(self, phase, depth, per_chunk, lhs):
        st, comm, par = self.stream, self.comm, self.n_ar % 2
        start = phase[0]
        ahead = start + st.n_slots
        stop = ahead + per_chunk * N_CHUNK

        @pl.loop(0, N_CHUNK)
        def _(k):
            for h in range(2):
                if per_chunk == 2 or h == 0:
                    slot = st.wait(phase, k * per_chunk + h)
                off = 0 if per_chunk == 2 else h * depth
                prod = jnp.dot(lhs[...], st.slots[slot, off:off + depth, :], preferred_element_type=F32).astype(BF)
                for r in range(2):
                    comm.part[k, r, :, h * TILE:(h + 1) * TILE] = prod[r * HALF:(r + 1) * HALF]
            for h in range(per_chunk):
                st.issue(ahead + k * per_chunk + h, ahead, stop)
            comm.copy1(par, k).start()

            @pl.when(k >= 1)
            def _():
                comm.chip_sum(par, k - 1)

        comm.chip_sum(par, N_CHUNK - 1)

    def mlp(self, up, down, layer, b1, b2, bd):
        st = self.stream
        start = up[0]
        ahead = start + st.n_slots
        stop = ahead + 24

        @pl.loop(0, 12)
        def _(i):
            s0 = st.wait(up, 2 * i)
            s1 = st.wait(up, 2 * i + 1)
            g = jnp.dot(self.n[...], st.slots[s0], preferred_element_type=F32)
            v = jnp.dot(self.n[...], st.slots[s1], preferred_element_type=F32)
            st.issue(ahead + 2 * i, ahead, stop)
            st.issue(ahead + 2 * i + 1, ahead, stop)
            g = g + f32(b1[layer:layer + 1, cols(i, TILE)])
            v = v + f32(b2[layer:layer + 1, cols(i, TILE)])
            self.hid[:, cols(i, TILE)] = (gelu(g) * v).astype(BF)

        self.down(down, 3072, 2, self.hid)
        self.all_reduce(bd, layer)


    def recurrent(self, x_tiles, mixed, y_tiles, out_tiles, layer, v, outs):
        st = self.stream
        ahead = x_tiles[0] + st.n_slots
        stop = ahead + 11

        @pl.loop(0, 5)
        def _(i):
            slot = st.wait(x_tiles, i)
            g = jnp.dot(self.n[...], st.slots[slot], preferred_element_type=F32)
            st.issue(ahead + i, ahead, stop)
            v.xb[:, cols(i, TILE)] = (g + f32(v.bx[layer:layer + 1, cols(i, TILE)])).astype(BF)

        slot = st.wait(mixed, 0)
        g = jnp.dot(self.n[...], st.slots[slot], preferred_element_type=F32)
        st.issue(ahead + 5, ahead, stop)
        v.xb[:, 1280:1408] = (g[:, 0:128] + f32(v.bx[layer:layer + 1, 1280:1408])).astype(BF)
        v.yg[:, 1280:1408] = gelu(g[:, 128:256] + f32(v.by[layer:layer + 1, 1280:1408]))

        outs.wait_inputs(layer)
        pos = v.tokc[...]

        @pl.loop(0, 11)
        def _(i):
            c = cols(i, 128)
            acc = f32(v.cb[layer:layer + 1, c]) + f32(v.cw[layer, 0:1, c]) * f32(v.xb[:, c])
            for j in range(3):
                acc = acc + jnp.where(pos >= 3 - j, f32(v.conv[layer, j, :, c]), 0.0) * f32(v.cw[layer, 3 - j:4 - j, c])
            v.xc[:, c] = acc.astype(BF)

        for b in range(8):
            c = slice(176 * b, 176 * (b + 1))
            xc = v.xc[:, c]
            v.rp[:, c] = jnp.dot(xc, v.ga[layer, b], preferred_element_type=F32)
            v.ip[:, c] = jnp.dot(xc, v.gi[layer, b], preferred_element_type=F32)

        def gate(c, reset):
            rate = -8.0 * jax.nn.softplus(v.ap[layer:layer + 1, c])
            decay = jnp.exp(rate * jax.nn.sigmoid(v.rp[:, c] + f32(v.gba[layer:layer + 1, c])))
            into = jnp.sqrt(1.0 - decay * decay)
            decay = jnp.where(reset, 0.0, decay)
            into = jnp.where(reset, 1.0, into)
            new = decay * v.lru[layer, :, c] + into * jax.nn.sigmoid(v.ip[:, c] + f32(v.gbi[layer:layer + 1, c])) * f32(v.xc[:, c])
            v.lru[layer, :, c] = new
            return new

        @pl.loop(0, 5)
        def _(i):
            slot = st.wait(y_tiles, i)
            g = jnp.dot(self.n[...], st.slots[slot], preferred_element_type=F32)
            st.issue(ahead + 6 + i, ahead, stop)
            for h in range(2):
                c = cols(2 * i + h, 128)
                new = gate(c, pos == 0)
                y = gelu(g[:, 128 * h:128 * (h + 1)] + f32(v.by[layer:layer + 1, c]))
                v.gated[:, c] = (new * y).astype(BF)

        c = slice(1280, 1408)
        v.gated[:, c] = (gate(c, pos == 0) * v.yg[:, c]).astype(BF)
        outs.write(layer)
        self.down(out_tiles, 1408, 1, v.gated)
        self.all_reduce(v.bout, layer)
        outs.wait_write(layer)


def add_mlp(stream, w1, w2, wd, layer):
    up = stream.add(24, columns(w1, layer, D), columns(w2, layer, D))
    return up, stream.add(16, columns(wd, layer, 3072))


class Names:
    def __init__(self, **kw):
        self.__dict__.update(kw)


class StateCopies:
    def __init__(self, ins, conv_out, lru_out, v, in_sem, out_sem):
        self.ins, self.conv_out, self.lru_out, self.v, self.in_sem, self.out_sem = ins, conv_out, lru_out, v, in_sem, out_sem

    def inputs(self, layer):
        return [pltpu.make_async_copy(src.at[layer], dst.at[layer], self.in_sem.at[layer, i]) for i, (src, dst) in enumerate(self.ins)]

    def start_inputs(self, layer):
        for c in self.inputs(layer):
            c.start()

    def wait_inputs(self, layer):
        for c in self.inputs(layer):
            c.wait()

    def outputs(self, layer):
        pairs = [(self.v.conv.at[layer, pl.ds(1, 2)], self.conv_out.at[layer, pl.ds(0, 2)]), (self.v.xb, self.conv_out.at[layer, 2]), (self.v.lru.at[layer], self.lru_out.at[layer])]
        return [pltpu.make_async_copy(src, dst, self.out_sem.at[layer, i]) for i, (src, dst) in enumerate(pairs)]

    def write(self, layer):
        for c in self.outputs(layer):
            c.start()

    def wait_write(self, layer):
        for c in self.outputs(layer):
            c.wait()


N_SLOTS_A = 21
N_SLOTS_B = 24
N_SLOTS_C = 26

COMM_SCRATCH = [
    pltpu.VMEM((N_CHUNK, 2, HALF, CHUNK), BF), pltpu.VMEM((N_CHUNK, HALF, CHUNK), BF), pltpu.VMEM((N_CHUNK, HALF, CHUNK), BF),
    pltpu.VMEM((2, N_CHUNK, HALF, CHUNK), BF), pltpu.VMEM((N_CHUNK, HALF, CHUNK), BF), pltpu.VMEM((N_CHUNK, HALF, CHUNK), BF),
] + [pltpu.SemaphoreType.DMA((2, N_CHUNK)) for _ in range(6)]


def body_scratch(n_slots, n_pieces):
    return [pltpu.VMEM((n_slots, D, TILE), BF), pltpu.SemaphoreType.DMA((n_slots, n_pieces)), pltpu.VMEM((ROWS, D), BF), pltpu.VMEM((ROWS, D), BF)]


def recurrent_kernel(tok, x_in, conv, lru, nscale, wx, bx, wy, by, cw, cb, ga, gba, gi, gbi, ap, wout, bout, w1, b1, w2, b2, wd, bd, *refs):
    x_out, conv_out, lru_out = refs[:3]
    slots, sems, x, n, hid, ss = refs[3:9]
    comm = Comm(*refs[9:21])
    small = refs[21:35]
    v_tok, v_ns, v_bx, v_by, v_cw, v_cb, v_gba, v_gbi, v_ap, v_bout, v_b1, v_b2, v_bd, small_sem = small
    v_conv, v_lru, v_ga, v_gi, xb, yg, xc, rp, ip, gated, tokc, in_sem, out_sem = refs[35:]
    stream = Stream(slots, sems, N_SLOTS_A)
    v = Names(bx=v_bx, by=v_by, cw=v_cw, cb=v_cb, ga=v_ga, gba=v_gba, gi=v_gi, gbi=v_gbi, ap=v_ap, bout=v_bout, conv=v_conv, lru=v_lru, xb=xb, yg=yg, xc=xc, rp=rp, ip=ip, gated=gated, tokc=tokc)
    outs = StateCopies([(conv, v_conv), (lru, v_lru), (ga, v_ga), (gi, v_gi)], conv_out, lru_out, v, in_sem, out_sem)
    body = Body(stream, comm, x, n, hid, ss, v_ns)

    plan = []
    for layer in range(2):
        xt = stream.add(5, columns(wx, layer, D))
        mixed = stream.add(1, lambda j, layer=layer: [(wx.at[layer, :, 1280:1408], (pl.ds(0, D), pl.ds(0, 128))), (wy.at[layer, :, 1280:1408], (pl.ds(0, D), pl.ds(128, 128)))])
        yt = stream.add(5, columns(wy, layer, D))
        ot = stream.add(8, lambda j, layer=layer: [(wout.at[layer, :, pl.ds(pl.multiple_of(j * CHUNK + h * TILE, TILE), TILE)], (pl.ds(h * 1408, 1408), pl.ds(0, TILE))) for h in range(2)])
        up, down = add_mlp(stream, w1, w2, wd, layer)
        plan.append((xt, mixed, yt, ot, up, down))

    pairs = [(x_in, x), (tok, v_tok), (nscale, v_ns), (bx, v_bx), (by, v_by), (cw, v_cw), (cb, v_cb), (gba, v_gba), (gbi, v_gbi), (ap, v_ap), (bout, v_bout), (b1, v_b1), (b2, v_b2), (bd, v_bd)]
    early = [pltpu.make_async_copy(s, d, small_sem.at[i]) for i, (s, d) in enumerate(pairs)]
    for c in early:
        c.start()
    stream.prime()
    outs.start_inputs(0)
    outs.start_inputs(1)
    comm.barrier()
    for c in early:
        c.wait()
    tokc[...] = jnp.broadcast_to(v_tok[...], (ROWS, 128)).T
    body.squares()
    for layer in range(2):
        xt, mixed, yt, ot, up, down = plan[layer]
        body.norm(2 * layer)
        body.recurrent(xt, mixed, yt, ot, layer, v, outs)
        body.norm(2 * layer + 1)
        body.mlp(up, down, layer, v_b1, v_b2, v_bd)
    last = pltpu.make_async_copy(x, x_out, small_sem.at[0])
    last.start()
    last.wait()


def final_kernel(x_in, part_in, nscale, bo, w1, b1, w2, b2, wd, bd, *refs):
    x_out = refs[0]
    slots, sems, x, n, hid, ss = refs[1:7]
    comm = Comm(*refs[7:19])
    v_ns, v_bo, v_b1, v_b2, v_bd, small_sem = refs[19:]
    stream = Stream(slots, sems, N_SLOTS_C)
    body = Body(stream, comm, x, n, hid, ss, v_ns)
    up, down = add_mlp(stream, w1, w2, wd, 2)
    pairs = [(part_in, comm.part), (x_in, x), (nscale, v_ns), (bo, v_bo), (b1, v_b1), (b2, v_b2), (bd, v_bd)]
    early = [pltpu.make_async_copy(s, d, small_sem.at[i]) for i, (s, d) in enumerate(pairs)]
    for c in early:
        c.start()
    stream.prime()
    comm.barrier()
    for c in early:
        c.wait()

    @pl.loop(0, N_CHUNK)
    def _(k):
        comm.copy1(0, k).start()

    @pl.loop(0, N_CHUNK)
    def _(k):
        comm.chip_sum(0, k)

    body.all_reduce(v_bo, 0)
    body.norm(5)
    body.mlp(up, down, 2, v_b1, v_b2, v_bd)
    last = pltpu.make_async_copy(x, x_out, small_sem.at[0])
    last.start()
    last.wait()


GROUP = 4
N_GROUP = ROWS // GROUP
WINDOW = 1024
HEADS = 8
LAG = 3


def attention_kernel(pos_s, tok, x_in, nscale, cosine, sine, k_cache, v_cache, slot_pos, wq, wk, wv, wo, part_out, k_out, v_out, slot_out,
                     slots, sems, x, n, ss, v_ns, v_tok, v_cos, v_sin, v_slot, bias, tokc, q3, o3, k_new, v_new, o_bf, part, small_sem, out_sem, slot_sem):
    stream = Stream(slots, sems, N_SLOTS_B)
    body = Body(stream, None, x, n, None, ss, v_ns)
    qt = stream.add(4, lambda j: [(wq.at[:, cols(j, TILE)], full(D))])
    kvt = stream.add(1, lambda j: [(wk, (pl.ds(0, D), pl.ds(0, 128))), (wv, (pl.ds(0, D), pl.ds(128, 128)))])

    def group_rows(j):
        return pl.ds(pl.multiple_of(j * GROUP * WINDOW, GROUP * WINDOW), GROUP * WINDOW)

    ct = stream.add(N_GROUP, lambda j: [(src.at[group_rows(j)], (pl.ds(0, D), pl.ds(128 * i, 128))) for i, src in enumerate((k_cache, v_cache))])
    ot = stream.add(4, lambda j: [(wo.at[:, cols(4 * j + h, TILE)], (pl.ds(1024 * h, 1024), pl.ds(0, TILE))) for h in range(4)])

    pairs = [(x_in, x), (tok, v_tok), (nscale, v_ns), (cosine, v_cos), (sine, v_sin), (slot_pos, v_slot)]
    early = [pltpu.make_async_copy(s, d, small_sem.at[i]) for i, (s, d) in enumerate(pairs)]
    for c in early:
        c.start()
    stream.prime()
    for c in early:
        c.wait()
    tokc[...] = jnp.broadcast_to(v_tok[...], (ROWS, 128)).T
    body.squares()
    body.norm(4)

    pos = tokc[...]
    target = lax.rem(pos, WINDOW)

    @pl.loop(0, WINDOW // 128)
    def _(i):
        lane = lax.broadcasted_iota(jnp.int32, (ROWS, 128), 1) + i * 128
        now = jnp.where(lane == target, pos, v_slot[:, cols(i, 128)])
        v_slot[:, cols(i, 128)] = now
        age = pos - now
        good = (now >= 0) & (age >= 0) & (age < WINDOW)
        bias[:, cols(i, 128)] = jnp.where(good, 0.0, -jnp.inf)

    slot_copy = pltpu.make_async_copy(v_slot, slot_out, slot_sem)
    slot_copy.start()

    lane = lax.broadcasted_iota(jnp.int32, (ROWS, 128), 1)

    def rope(val):
        other = jnp.where(lane < 32, pltpu.roll(val, 96, 1), pltpu.roll(val, 32, 1))
        return val * v_cos[...] + other * v_sin[...]

    ahead = stream.n_slots
    for j in range(4):
        slot = stream.wait(qt, j)
        g = jnp.dot(n[...], slots[slot], preferred_element_type=F32)
        stream.issue(ahead + j, ahead, ahead + 5)
        for h in range(2):
            q3[pl.ds(2 * j + h, ROWS, stride=HEADS), :] = f32(rope(g[:, 128 * h:128 * (h + 1)]).astype(BF))
    slot = stream.wait(kvt, 0)
    g = jnp.dot(n[...], slots[slot], preferred_element_type=F32)
    stream.issue(ahead + 4, ahead, ahead + 5)
    k_new[...] = f32(rope(g[:, 0:128]).astype(BF))
    v_new[...] = f32(g[:, 128:256].astype(BF))

    def outputs(j):
        slot = stream.slot_of(ct[0] + j)
        return [pltpu.make_async_copy(slots.at[slot, :, pl.ds(128 * i, 128)], dst.at[group_rows(j)], out_sem.at[slot, i]) for i, dst in enumerate((k_out, v_out))]

    row16 = lax.broadcasted_iota(jnp.int32, (16, 128), 0)
    ahead = ct[0] - LAG + stream.n_slots

    @pl.loop(0, N_GROUP)
    def _(j):
        slot = stream.wait(ct, j)
        for r in range(GROUP):
            seq = j * GROUP + r
            spot = lax.rem(pos_s[seq], WINDOW)
            base = pl.multiple_of(r * WINDOW + lax.div(spot, 16) * 16, 16)
            for i, new in enumerate((k_new, v_new)):
                here = (slot, pl.ds(base, 16), pl.ds(128 * i, 128))
                slots[here] = jnp.where(row16 == lax.rem(spot, 16), new[pl.ds(seq, 1), :], f32(slots[here])).astype(BF)
        for c in outputs(j):
            c.start()
        for r in range(GROUP):
            seq = j * GROUP + r
            q = q3[pl.ds(pl.multiple_of(seq * HEADS, HEADS), HEADS), :].astype(BF)
            keys = slots[slot, r * WINDOW:(r + 1) * WINDOW, 0:128]
            score = lax.dot_general(q, keys, (((1,), (1,)), ((), ())), preferred_element_type=F32) * (128 ** -0.5)
            score = score + bias[pl.ds(seq, 1), :]
            p = jnp.exp(score - jnp.max(score, axis=-1, keepdims=True))
            p = (p / jnp.sum(p, axis=-1, keepdims=True)).astype(BF)
            o = jnp.dot(p, slots[slot, r * WINDOW:(r + 1) * WINDOW, 128:256], preferred_element_type=F32)
            o3[pl.ds(pl.multiple_of(seq * HEADS, HEADS), HEADS), :] = o

        @pl.when(j >= LAG)
        def _():
            for c in outputs(j - LAG):
                c.wait()
            stream.issue(ahead + j, ahead + LAG, ahead + N_GROUP)

    for h in range(HEADS):
        o_bf[:, 128 * h:128 * (h + 1)] = o3[pl.ds(h, ROWS, stride=HEADS), :].astype(BF)

    @pl.loop(0, 4)
    def _(j):
        slot = stream.wait(ot, j)
        for h in range(4):
            prod = jnp.dot(o_bf[...], slots[slot, 1024 * h:1024 * (h + 1), :], preferred_element_type=F32).astype(BF)
            for r in range(2):
                part[2 * j + h // 2, r, :, (h % 2) * TILE:(h % 2 + 1) * TILE] = prod[r * HALF:(r + 1) * HALF]

    last = pltpu.make_async_copy(part, part_out, small_sem.at[0])
    last.start()
    for j in range(N_GROUP - LAG, N_GROUP):
        for c in outputs(j):
            c.wait()
    slot_copy.wait()
    last.wait()


ANY = pl.BlockSpec(memory_space=pl.ANY)


def rope_tables(tok_pos):
    quarter = 32
    inv_freq = ROPE_BASE ** (-jnp.arange(quarter, dtype=F32) / quarter)
    angles = tok_pos.astype(F32)[:, None] * inv_freq[None, :]
    cosine, sine = jnp.cos(angles), jnp.sin(angles)
    rows = tok_pos.shape[0]
    return (jnp.concatenate([cosine, cosine, jnp.ones((rows, 64), F32)], axis=1), jnp.concatenate([-sine, sine, jnp.zeros((rows, 64), F32)], axis=1))


def io_specs():
    in_specs = (P('dp', None), P('dp'), P(None, 'dp', None, 'tp'), P(None, 'dp', 'tp'), P('dp', None, None), P('dp', None, None), P('dp', None),
                P(), P(None, None, 'tp'), P(None, 'tp'), P(None, None, 'tp'), P(None, 'tp'), P(None, None, 'tp'), P(None, 'tp'),
                P(None, 'tp', None, None), P(None, 'tp'), P(None, 'tp', None, None), P(None, 'tp'), P(None, 'tp'), P(None, 'tp', None), P(),
                P(None, 'tp'), P(), P(), P('tp', None), P(),
                P(None, None, 'tp'), P(None, 'tp'), P(None, None, 'tp'), P(None, 'tp'), P(None, 'tp', None), P())
    out_specs = (P('dp', None), P(None, 'dp', None, 'tp'), P(None, 'dp', 'tp'), P('dp', None, None), P('dp', None, None), P('dp', None))
    return in_specs, out_specs


def solution(mesh):
    in_specs, out_specs = io_specs()
    shape = jax.ShapeDtypeStruct

    def local_step(x_in, tok_pos, conv_state, lru_state, k_cache, v_cache, slot_pos, norm_scale, rec_wx, rec_bx, rec_wy, rec_by, conv_w, conv_b, gate_wa, gate_ba, gate_wi, gate_bi, a_param, rec_wout, rec_bout, attn_wq, attn_wk, attn_wv, attn_wo, attn_bo, mlp_w1, mlp_b1, mlp_w2, mlp_b2, mlp_wd, mlp_bd):
        tok = tok_pos.reshape(1, ROWS)
        scales = norm_scale.reshape(6, D)
        cosine, sine = rope_tables(tok_pos)
        vec = pltpu.VMEM((2, 1408), BF)
        x_mid, conv_out, lru_out = pl.pallas_call(
            recurrent_kernel,
            out_shape=[shape((ROWS, D), BF), shape((2, 3, ROWS, 1408), BF), shape((2, ROWS, 1408), F32)],
            in_specs=[ANY] * 24, out_specs=[ANY] * 3,
            scratch_shapes=body_scratch(N_SLOTS_A, 2) + [pltpu.VMEM((ROWS, 3072), BF), pltpu.VMEM((ROWS, 128), F32)] + COMM_SCRATCH + [
                pltpu.VMEM((1, ROWS), jnp.int32), pltpu.VMEM((6, D), BF), vec, vec, pltpu.VMEM((2, 4, 1408), BF), vec, vec, vec, pltpu.VMEM((2, 1408), F32),
                pltpu.VMEM((2, D), BF), pltpu.VMEM((3, 3072), BF), pltpu.VMEM((3, 3072), BF), pltpu.VMEM((3, D), BF), pltpu.SemaphoreType.DMA((14,)),
                pltpu.VMEM((2, 3, ROWS, 1408), BF), pltpu.VMEM((2, ROWS, 1408), F32), pltpu.VMEM((2, 8, 176, 176), BF), pltpu.VMEM((2, 8, 176, 176), BF),
                pltpu.VMEM((ROWS, 1408), BF), pltpu.VMEM((ROWS, 1408), F32), pltpu.VMEM((ROWS, 1408), BF), pltpu.VMEM((ROWS, 1408), F32), pltpu.VMEM((ROWS, 1408), F32),
                pltpu.VMEM((ROWS, 1408), BF), pltpu.VMEM((ROWS, 128), jnp.int32), pltpu.SemaphoreType.DMA((2, 4)), pltpu.SemaphoreType.DMA((2, 3))],
            compiler_params=pltpu.CompilerParams(collective_id=0, has_side_effects=True, vmem_limit_bytes=VMEM_LIMIT),
            name='recurrent_layers',
        )(tok, x_in, jnp.transpose(conv_state, (0, 2, 1, 3)), lru_state, scales, rec_wx, rec_bx, rec_wy, rec_by, conv_w, conv_b, gate_wa, gate_ba, gate_wi, gate_bi, a_param, rec_wout, rec_bout, mlp_w1, mlp_b1, mlp_w2, mlp_b2, mlp_wd, mlp_bd)
        cache = (ROWS * WINDOW, 128)
        table = pltpu.VMEM((ROWS, 128), F32)
        part, k_out, v_out, slot_out = pl.pallas_call(
            attention_kernel,
            out_shape=[shape((N_CHUNK, 2, HALF, CHUNK), BF), shape(cache, BF), shape(cache, BF), shape((ROWS, WINDOW), jnp.int32)],
            in_specs=[pl.BlockSpec(memory_space=pltpu.SMEM)] + [ANY] * 12, out_specs=[ANY] * 4,
            scratch_shapes=body_scratch(N_SLOTS_B, 4) + [
                table, pltpu.VMEM((6, D), BF), pltpu.VMEM((1, ROWS), jnp.int32), table, table, pltpu.VMEM((ROWS, WINDOW), jnp.int32), pltpu.VMEM((ROWS, WINDOW), F32),
                pltpu.VMEM((ROWS, 128), jnp.int32), pltpu.VMEM((ROWS * HEADS, 128), F32), pltpu.VMEM((ROWS * HEADS, 128), F32), table, table,
                pltpu.VMEM((ROWS, 1024), BF), pltpu.VMEM((N_CHUNK, 2, HALF, CHUNK), BF), pltpu.SemaphoreType.DMA((6,)), pltpu.SemaphoreType.DMA((N_SLOTS_B, 2)), pltpu.SemaphoreType.DMA],
            compiler_params=pltpu.CompilerParams(vmem_limit_bytes=VMEM_LIMIT),
            name='attention_layer',
        )(tok_pos, tok, x_mid, scales, cosine, sine, k_cache.reshape(cache), v_cache.reshape(cache), slot_pos, attn_wq, attn_wk, attn_wv, attn_wo)
        x_out = pl.pallas_call(
            final_kernel,
            out_shape=shape((ROWS, D), BF),
            in_specs=[ANY] * 10, out_specs=ANY,
            scratch_shapes=body_scratch(N_SLOTS_C, 1) + [pltpu.VMEM((ROWS, 3072), BF), pltpu.VMEM((ROWS, 128), F32)] + COMM_SCRATCH + [
                pltpu.VMEM((6, D), BF), pltpu.VMEM((1, D), BF), pltpu.VMEM((3, 3072), BF), pltpu.VMEM((3, 3072), BF), pltpu.VMEM((3, D), BF), pltpu.SemaphoreType.DMA((7,))],
            compiler_params=pltpu.CompilerParams(collective_id=1, has_side_effects=True, vmem_limit_bytes=VMEM_LIMIT),
            name='last_mlp',
        )(x_mid, part, scales, attn_bo.reshape(1, D), mlp_w1, mlp_b1, mlp_w2, mlp_b2, mlp_wd, mlp_bd)
        return (x_out, jnp.transpose(conv_out, (0, 2, 1, 3)), lru_out, k_out.reshape(k_cache.shape), v_out.reshape(v_cache.shape), slot_out)

    return jax.shard_map(local_step, mesh=mesh, in_specs=in_specs, out_specs=out_specs, check_vma=False)
```

time: 477 us -> 237 us (0.50); the launches traced: 469 us -> 237 us
  Pallas kernels: 0 us -> 223 us
  matrix products: 177 us -> 0 us
  waiting for transfers between devices: 174 us -> 0 us
  other arithmetic: 89.2 us -> 1.72 us
  between operations: 15.3 us -> 0.67 us
    pallas_call x0 -> x3, Pallas kernels: none -> 223 us  [the longest x1 112 us: local_step(): pl.pallas_call(recurrent_kernel, out_shape=[shape((ROWS, D), BF), shape((...]
    dot_general x20 -> x0, matrix products: 177 us -> none  [the longest x3 59 us: mlp_update(): return jnp.dot(hidden, w_down, preferred_element_type=jnp.float32)]
    psum x6 -> x0, waiting for transfers between devices: 174 us -> none  [local_step(): lax.psum(part_sum.astype(jnp.bfloat16), 'tp')]
    select_n x1 -> x0, other arithmetic: 44.3 us -> none  [write_cache(): k_next = jnp.where(target[:, :, None], k_new[:, None, :], k_cache)]
    reduce_sum x7 -> x0, other arithmetic: 14.2 us -> none  [the longest x6 10.9 us: rms_norm(): mean_sq = jnp.mean(res_f * res_f, axis=-1, keepdims=True)]
    add x11 -> x0, other arithmetic: 13 us -> none  [the longest x2 5.19 us: recurrent_update(): decay_gate * lru_prev]
    another operation x5 -> x0, other arithmetic: 6.34 us -> none  [the longest x3 3.74 us: local_step(): jnp.stack(conv_list)]
    unnamed x91 -> x3, local copies, waits for them, and re-layouts: 1.94 us -> 7.95 us
  transfers between devices with their start and end apart: 6 -> 0, of which waited for: 6 -> 0; matrix products, arithmetic and copies ran while one was open for 3% -> 0% of each run, Pallas kernels for 0% -> 0%
where the time goes in v1:
time: 237 us
  Pallas kernels  223 us (94%)
  local copies, waits for them, and re-layouts  10.9 us (5%)
    pallas_call x1, Pallas kernels, local_step(): pl.pallas_call(recurrent_kernel, out_shape=[shape((ROWS, D), BF), shape((...  112 us
    pallas_call x1, Pallas kernels, local_step(): pl.pallas_call(attention_kernel, out_shape=[shape((N_CHUNK, 2, HALF, CHUN...  64.6 us
    pallas_call x1, Pallas kernels, local_step(): pl.pallas_call(final_kernel, out_shape=shape((ROWS, D), BF), in_specs=[AN...  47.1 us
    unnamed x3, local copies, waits for them, and re-layouts  7.95 us

profile of v1, /device:TPU:0, one launch (start us, length us, event | category | flops | bytes accessed | tf_op | source)
XLA Modules:
  0.0 236.6 jit_solution(8755517557640700215)
XLA Ops:
  0.6 0.7 convert_element_type.3
  1.3 0.1 pad.5.clone
  1.4 0.1 pad.2.clone
  1.5 1.3 reshape.44.bo
  2.8 1.5 reshape.41.nscale
  4.2 0.3 fusion
  4.5 0.7 maximum_maximum_fusion
  5.3 111.7 %recurrent_layers.1 = (bf16[128,4096]{1,0:T(8,128)(2,1)}, bf16[2,3,128,1408]{3,2,1,0:T(8,128)(2,1)}, f32[2,128,1408]{2,1,0:T(8,128)}) custom-call(s32[1,128]{1,0:T(1,128)} %bitcast.11, bf16[128,4096]{1,0:T(8,128)(2,1)} %x_in.1, bf16[2,3,128,1408]{3,2,1,0:T(8,128)(2,1)} %bitcast.9, f32[2,128,1408]{2,1,0:T(8,128)} %lru.1, bf16[6,4096]{1,0:T(8,128)(2,1)} %reshape.41.nscale, ...), custom_call_target="tpu_custom_call" | custom-call | tf_op jit(solution)/shard_map/recurrent_layers/pallas_call | solution.py:591
  117.0 64.6 %attention_layer.1 = (bf16[8,2,64,512]{3,2,1,0:T(8,128)(2,1)}, bf16[131072,128]{1,0:T(8,128)(2,1)}, bf16[131072,128]{1,0:T(8,128)(2,1)}, s32[128,1024]{1,0:T(8,128)}) custom-call(s32[128]{0:T(128)} %pos_s.1, s32[1,128]{1,0:T(1,128)} %bitcast.12, bf16[128,4096]{1,0:T(8,128)(2,1)} %get-tuple-element.13.x_in, bf16[6,4096]{1,0:T(8,128)(2,1)} %reshape.41.nscale, ...), custom_call_target="tpu_custom_call" | custom-call | tf_op jit(solution)/shard_map/attention_layer/pallas_call | solution.py:606
  181.6 47.1 %last_mlp.1 = bf16[128,4096]{1,0:T(8,128)(2,1)} custom-call(bf16[128,4096]{1,0:T(8,128)(2,1)} %get-tuple-element.13.x_in, bf16[8,2,64,512]{3,2,1,0:T(8,128)(2,1)} %get-tuple-element.14.part_in, bf16[6,4096]{1,0:T(8,128)(2,1)} %reshape.41.nscale, bf16[1,4096]{1,0:T(2,128)(2,1)} %reshape.44.bo, bf16[3,4096,3072]{2,1,0:T(8,128)(2,1)} %w1.3, ...), custom_call_target="tpu_custom_call" | custom-call | tf_op jit(solution)/shard_map/last_mlp/pallas_call | solution.py:617
  228.6 2.3 copy.42
  230.9 3.1 %copy.43 = bf16[2,128,3,1408]{3,1,2,0:T(8,128)(2,1)} copy(bf16[2,128,3,1408]{3,1,2,0:T(8,128)(2,1)} %bitcast.10) | data formatting | bytes 4325376
  234.0 2.6 %copy.44 = f32[2,128,1408]{2,1,0:T(8,128)} copy(f32[2,128,1408]{2,1,0:T(8,128)} %get-tuple-element.33) | data formatting | bytes 2883584
  (3 shorter events, 0.0 us)

commit v2 on v1

--- a/solution.py
+++ b/solution.py
@@ -1,5 +1,6 @@
 import jax
 import jax.numpy as jnp
+import numpy as np
 from jax import lax
 from jax.experimental import pallas as pl
 from jax.experimental.pallas import tpu as pltpu
@@ -108,11 +109,12 @@
         self.partner = me + 1 - 2 * self.mine
         self.peer = lax.rem(me + 2, 4)
 
-    def barrier(self):
-        sem = pltpu.get_barrier_semaphore()
+    def greet(self):
         for dev in (self.partner, self.peer):
-            pl.semaphore_signal(sem, inc=1, device_id={'tp': dev}, device_id_type=pl.DeviceIdType.MESH)
-        pl.semaphore_wait(sem, 2)
+            pl.semaphore_signal(pltpu.get_barrier_semaphore(), inc=1, device_id={'tp': dev}, device_id_type=pl.DeviceIdType.MESH)
+
+    def meet(self):
+        pl.semaphore_wait(pltpu.get_barrier_semaphore(), 2)
 
     def copy1(self, par, k):
         return pltpu.make_async_remote_copy(src_ref=self.part.at[k, self.other], dst_ref=self.r1.at[k], send_sem=self.s1.at[par, k], recv_sem=self.q1.at[par, k], device_id={'tp': self.partner}, device_id_type=pl.DeviceIdType.MESH)
@@ -177,13 +179,13 @@
 
         @pl.loop(0, N_CHUNK)
         def _(k):
-            gain = 1.0 + f32(self.nscale[row:row + 1, cols(k)])
+            gain = 1.0 + f32(self.nscale[row // 2, row % 2:row % 2 + 1, cols(k)])
             self.n[:, cols(k)] = (f32(self.x[:, cols(k)]) * scale * gain).astype(BF)
 
     def updater(self, bias, row):
         def update(half, k, u):
             rows = pl.ds(pl.multiple_of(half * HALF, HALF), HALF)
-            new = (f32(self.x[rows, cols(k)]) + u + f32(bias[row:row + 1, cols(k)])).astype(BF)
+            new = (f32(self.x[rows, cols(k)]) + u + f32(bias[cols(k)].reshape(1, CHUNK) if row is None else bias[row:row + 1, cols(k)])).astype(BF)
             self.x[rows, cols(k)] = new
             v = f32(new)
             self.ss[rows, :] += fold_lanes(v * v)
@@ -248,18 +250,29 @@
         ahead = x_tiles[0] + st.n_slots
         stop = ahead + 11
 
-        @pl.loop(0, 5)
-        def _(i):
-            slot = st.wait(x_tiles, i)
-            g = jnp.dot(self.n[...], st.slots[slot], preferred_element_type=F32)
-            st.issue(ahead + i, ahead, stop)
-            v.xb[:, cols(i, TILE)] = (g + f32(v.bx[layer:layer + 1, cols(i, TILE)])).astype(BF)
-
-        slot = st.wait(mixed, 0)
-        g = jnp.dot(self.n[...], st.slots[slot], preferred_element_type=F32)
-        st.issue(ahead + 5, ahead, stop)
-        v.xb[:, 1280:1408] = (g[:, 0:128] + f32(v.bx[layer:layer + 1, 1280:1408])).astype(BF)
-        v.yg[:, 1280:1408] = gelu(g[:, 128:256] + f32(v.by[layer:layer + 1, 1280:1408]))
+        def dots(phase, tiles):
+            slots = [st.wait(phase, i) for i in tiles]
+            return [jnp.dot(self.n[...], st.slots[slot], preferred_element_type=F32) for slot in slots]
+
+        def put_x(i, g):
+            v.xb[layer, :, cols(i, TILE)] = (g + f32(v.bx[layer:layer + 1, cols(i, TILE)])).astype(BF)
+
+        @pl.loop(0, 2)
+        def _(p):
+            for h, g in enumerate(dots(x_tiles, [2 * p, 2 * p + 1])):
+                put_x(2 * p + h, g)
+            for h in range(2):
+                st.issue(ahead + 2 * p + h, ahead, stop)
+
+        if layer == 0:
+            self.comm.meet()
+        last_x, = dots(x_tiles, [4])
+        g, = dots(mixed, [0])
+        for h in range(2):
+            st.issue(ahead + 4 + h, ahead, stop)
+        put_x(4, last_x)
+        v.xb[layer, :, 1280:1408] = (g[:, 0:128] + f32(v.bx[layer:layer + 1, 1280:1408])).astype(BF)
+        v.yg[...] = gelu(g[:, 128:256] + f32(v.by[layer:layer + 1, 1280:1408]))
 
         outs.wait_inputs(layer)
         pos = v.tokc[...]
@@ -267,7 +280,7 @@
         @pl.loop(0, 11)
         def _(i):
             c = cols(i, 128)
-            acc = f32(v.cb[layer:layer + 1, c]) + f32(v.cw[layer, 0:1, c]) * f32(v.xb[:, c])
+            acc = f32(v.cb[layer:layer + 1, c]) + f32(v.cw[layer, 0:1, c]) * f32(v.xb[layer, :, c])
             for j in range(3):
                 acc = acc + jnp.where(pos >= 3 - j, f32(v.conv[layer, j, :, c]), 0.0) * f32(v.cw[layer, 3 - j:4 - j, c])
             v.xc[:, c] = acc.astype(BF)
@@ -288,19 +301,25 @@
             v.lru[layer, :, c] = new
             return new
 
-        @pl.loop(0, 5)
-        def _(i):
-            slot = st.wait(y_tiles, i)
-            g = jnp.dot(self.n[...], st.slots[slot], preferred_element_type=F32)
-            st.issue(ahead + 6 + i, ahead, stop)
+        def put_y(i, g):
             for h in range(2):
                 c = cols(2 * i + h, 128)
                 new = gate(c, pos == 0)
                 y = gelu(g[:, 128 * h:128 * (h + 1)] + f32(v.by[layer:layer + 1, c]))
                 v.gated[:, c] = (new * y).astype(BF)
 
+        @pl.loop(0, 2)
+        def _(p):
+            for h, g in enumerate(dots(y_tiles, [2 * p, 2 * p + 1])):
+                put_y(2 * p + h, g)
+            for h in range(2):
+                st.issue(ahead + 6 + 2 * p + h, ahead, stop)
+
+        g, = dots(y_tiles, [4])
+        st.issue(ahead + 10, ahead, stop)
+        put_y(4, g)
         c = slice(1280, 1408)
-        v.gated[:, c] = (gate(c, pos == 0) * v.yg[:, c]).astype(BF)
+        v.gated[:, c] = (gate(c, pos == 0) * v.yg[...]).astype(BF)
         outs.write(layer)
         self.down(out_tiles, 1408, 1, v.gated)
         self.all_reduce(v.bout, layer)
@@ -318,8 +337,8 @@
 
 
 class StateCopies:
-    def __init__(self, ins, conv_out, lru_out, v, in_sem, out_sem):
-        self.ins, self.conv_out, self.lru_out, self.v, self.in_sem, self.out_sem = ins, conv_out, lru_out, v, in_sem, out_sem
+    def __init__(self, ins, xb_out, lru_out, v, in_sem, out_sem):
+        self.ins, self.xb_out, self.lru_out, self.v, self.in_sem, self.out_sem = ins, xb_out, lru_out, v, in_sem, out_sem
 
     def inputs(self, layer):
         return [pltpu.make_async_copy(src.at[layer], dst.at[layer], self.in_sem.at[layer, i]) for i, (src, dst) in enumerate(self.ins)]
@@ -333,7 +352,7 @@
             c.wait()
 
     def outputs(self, layer):
-        pairs = [(self.v.conv.at[layer, pl.ds(1, 2)], self.conv_out.at[layer, pl.ds(0, 2)]), (self.v.xb, self.conv_out.at[layer, 2]), (self.v.lru.at[layer], self.lru_out.at[layer])]
+        pairs = [(self.v.xb.at[layer], self.xb_out.at[layer]), (self.v.lru.at[layer], self.lru_out.at[layer])]
         return [pltpu.make_async_copy(src, dst, self.out_sem.at[layer, i]) for i, (src, dst) in enumerate(pairs)]
 
     def write(self, layer):
@@ -345,9 +364,9 @@
             c.wait()
 
 
-N_SLOTS_A = 21
-N_SLOTS_B = 24
-N_SLOTS_C = 26
+N_SLOTS_A = 20
+N_SLOTS_B = 22
+N_SLOTS_C = 24
 
 COMM_SCRATCH = [
     pltpu.VMEM((N_CHUNK, 2, HALF, CHUNK), BF), pltpu.VMEM((N_CHUNK, HALF, CHUNK), BF), pltpu.VMEM((N_CHUNK, HALF, CHUNK), BF),
@@ -360,7 +379,7 @@
 
 
 def recurrent_kernel(tok, x_in, conv, lru, nscale, wx, bx, wy, by, cw, cb, ga, gba, gi, gbi, ap, wout, bout, w1, b1, w2, b2, wd, bd, *refs):
-    x_out, conv_out, lru_out = refs[:3]
+    x_out, xb_out, lru_out = refs[:3]
     slots, sems, x, n, hid, ss = refs[3:9]
     comm = Comm(*refs[9:21])
     small = refs[21:35]
@@ -368,7 +387,7 @@
     v_conv, v_lru, v_ga, v_gi, xb, yg, xc, rp, ip, gated, tokc, in_sem, out_sem = refs[35:]
     stream = Stream(slots, sems, N_SLOTS_A)
     v = Names(bx=v_bx, by=v_by, cw=v_cw, cb=v_cb, ga=v_ga, gba=v_gba, gi=v_gi, gbi=v_gbi, ap=v_ap, bout=v_bout, conv=v_conv, lru=v_lru, xb=xb, yg=yg, xc=xc, rp=rp, ip=ip, gated=gated, tokc=tokc)
-    outs = StateCopies([(conv, v_conv), (lru, v_lru), (ga, v_ga), (gi, v_gi)], conv_out, lru_out, v, in_sem, out_sem)
+    outs = StateCopies([(conv, v_conv), (lru, v_lru), (ga, v_ga), (gi, v_gi)], xb_out, lru_out, v, in_sem, out_sem)
     body = Body(stream, comm, x, n, hid, ss, v_ns)
 
     plan = []
@@ -384,10 +403,10 @@
     early = [pltpu.make_async_copy(s, d, small_sem.at[i]) for i, (s, d) in enumerate(pairs)]
     for c in early:
         c.start()
+    comm.greet()
     stream.prime()
     outs.start_inputs(0)
     outs.start_inputs(1)
-    comm.barrier()
     for c in early:
         c.wait()
     tokc[...] = jnp.broadcast_to(v_tok[...], (ROWS, 128)).T
@@ -404,10 +423,9 @@
 
 
 def final_kernel(x_in, part_in, nscale, bo, w1, b1, w2, b2, wd, bd, *refs):
-    x_out = refs[0]
-    slots, sems, x, n, hid, ss = refs[1:7]
-    comm = Comm(*refs[7:19])
-    v_ns, v_bo, v_b1, v_b2, v_bd, small_sem = refs[19:]
+    x, slots, sems, n, hid, ss = refs[:6]
+    comm = Comm(*refs[6:18])
+    v_ns, v_bo, v_b1, v_b2, v_bd, small_sem = refs[18:]
     stream = Stream(slots, sems, N_SLOTS_C)
     body = Body(stream, comm, x, n, hid, ss, v_ns)
     up, down = add_mlp(stream, w1, w2, wd, 2)
@@ -415,36 +433,38 @@
     early = [pltpu.make_async_copy(s, d, small_sem.at[i]) for i, (s, d) in enumerate(pairs)]
     for c in early:
         c.start()
+    comm.greet()
     stream.prime()
-    comm.barrier()
-    for c in early:
-        c.wait()
+    early[0].wait()
+    comm.meet()
 
     @pl.loop(0, N_CHUNK)
     def _(k):
         comm.copy1(0, k).start()
 
+    for c in early[1:]:
+        c.wait()
+
     @pl.loop(0, N_CHUNK)
     def _(k):
         comm.chip_sum(0, k)
 
-    body.all_reduce(v_bo, 0)
+    body.all_reduce(v_bo, None)
     body.norm(5)
     body.mlp(up, down, 2, v_b1, v_b2, v_bd)
-    last = pltpu.make_async_copy(x, x_out, small_sem.at[0])
-    last.start()
-    last.wait()
 
 
 GROUP = 4
 N_GROUP = ROWS // GROUP
 WINDOW = 1024
 HEADS = 8
-LAG = 3
-
-
-def attention_kernel(pos_s, tok, x_in, nscale, cosine, sine, k_cache, v_cache, slot_pos, wq, wk, wv, wo, part_out, k_out, v_out, slot_out,
-                     slots, sems, x, n, ss, v_ns, v_tok, v_cos, v_sin, v_slot, bias, tokc, q3, o3, k_new, v_new, o_bf, part, small_sem, out_sem, slot_sem):
+LAG = 4
+FREQ = np.zeros((1, 128), np.float32)
+FREQ[0, :32] = FREQ[0, 32:64] = np.float32(ROPE_BASE) ** (-np.arange(32, dtype=np.float32) / 32)
+
+
+def attention_kernel(pos_s, tok, x_in, nscale, freq, conv, xb, lru, k_cache, v_cache, slot_pos, wq, wk, wv, wo, part_out, conv_out, lru_out, k_out, v_out, slot_out,
+                     slots, sems, x, n, ss, v_ns, v_tok, v_freq, v_cos, v_sin, v_conv, v_lru, v_slot, bias, tokc, q3, o3, k_new, v_new, o_bf, part, small_sem, state_sem, out_sem):
     stream = Stream(slots, sems, N_SLOTS_B)
     body = Body(stream, None, x, n, None, ss, v_ns)
     qt = stream.add(4, lambda j: [(wq.at[:, cols(j, TILE)], full(D))])
@@ -456,50 +476,67 @@
     ct = stream.add(N_GROUP, lambda j: [(src.at[group_rows(j)], (pl.ds(0, D), pl.ds(128 * i, 128))) for i, src in enumerate((k_cache, v_cache))])
     ot = stream.add(4, lambda j: [(wo.at[:, cols(4 * j + h, TILE)], (pl.ds(1024 * h, 1024), pl.ds(0, TILE))) for h in range(4)])
 
-    pairs = [(x_in, x), (tok, v_tok), (nscale, v_ns), (cosine, v_cos), (sine, v_sin), (slot_pos, v_slot)]
-    early = [pltpu.make_async_copy(s, d, small_sem.at[i]) for i, (s, d) in enumerate(pairs)]
-    for c in early:
-        c.start()
+    def copies(pairs, sem):
+        return [pltpu.make_async_copy(a, b, sem.at[i]) for i, (a, b) in enumerate(pairs)]
+
+    def start(group):
+        for c in group:
+            c.start()
+
+    def finish(group):
+        for c in group:
+            c.wait()
+
+    early = copies([(x_in, x), (tok, v_tok), (nscale, v_ns), (freq, v_freq), (slot_pos, v_slot)], small_sem)
+    start(early)
     stream.prime()
-    for c in early:
-        c.wait()
+    states = copies([(conv.at[:, 1:3], v_conv.at[:, 0:2]), (xb, v_conv.at[:, 2]), (lru, v_lru)], state_sem)
+    start(states)
+    finish(early)
     tokc[...] = jnp.broadcast_to(v_tok[...], (ROWS, 128)).T
     body.squares()
     body.norm(4)
 
     pos = tokc[...]
     target = lax.rem(pos, WINDOW)
+    lane = lax.broadcasted_iota(jnp.int32, (ROWS, 128), 1)
+    angle = f32(pos) * v_freq[...]
+    v_cos[...] = jnp.cos(angle)
+    v_sin[...] = jnp.sin(angle) * jnp.where(lane < 32, -1.0, 1.0)
 
     @pl.loop(0, WINDOW // 128)
     def _(i):
-        lane = lax.broadcasted_iota(jnp.int32, (ROWS, 128), 1) + i * 128
-        now = jnp.where(lane == target, pos, v_slot[:, cols(i, 128)])
+        now = jnp.where(lane + i * 128 == target, pos, v_slot[:, cols(i, 128)])
         v_slot[:, cols(i, 128)] = now
         age = pos - now
         good = (now >= 0) & (age >= 0) & (age < WINDOW)
         bias[:, cols(i, 128)] = jnp.where(good, 0.0, -jnp.inf)
 
-    slot_copy = pltpu.make_async_copy(v_slot, slot_out, slot_sem)
-    slot_copy.start()
-
-    lane = lax.broadcasted_iota(jnp.int32, (ROWS, 128), 1)
-
     def rope(val):
         other = jnp.where(lane < 32, pltpu.roll(val, 96, 1), pltpu.roll(val, 32, 1))
         return val * v_cos[...] + other * v_sin[...]
 
     ahead = stream.n_slots
-    for j in range(4):
-        slot = stream.wait(qt, j)
-        g = jnp.dot(n[...], slots[slot], preferred_element_type=F32)
-        stream.issue(ahead + j, ahead, ahead + 5)
-        for h in range(2):
-            q3[pl.ds(2 * j + h, ROWS, stride=HEADS), :] = f32(rope(g[:, 128 * h:128 * (h + 1)]).astype(BF))
+
+    @pl.loop(0, 2)
+    def _(p):
+        got = [stream.wait(qt, 2 * p + i) for i in range(2)]
+        for i, slot in enumerate(got):
+            g = jnp.dot(n[...], slots[slot], preferred_element_type=F32)
+            for h in range(2):
+                q3[pl.ds(4 * p + 2 * i + h, ROWS, stride=HEADS), :] = f32(rope(g[:, 128 * h:128 * (h + 1)]).astype(BF))
+        for i in range(2):
+            stream.issue(ahead + 2 * p + i, ahead, ahead + 4)
+
     slot = stream.wait(kvt, 0)
     g = jnp.dot(n[...], slots[slot], preferred_element_type=F32)
-    stream.issue(ahead + 4, ahead, ahead + 5)
+    stream.issue(ahead + 4, ahead + 4, ahead + 5)
     k_new[...] = f32(rope(g[:, 0:128]).astype(BF))
     v_new[...] = f32(g[:, 128:256].astype(BF))
+
+    finish(states)
+    results = copies([(v_conv, conv_out), (v_lru, lru_out), (v_slot, slot_out)], state_sem)
+    start(results)
 
     def outputs(j):
         slot = stream.slot_of(ct[0] + j)
@@ -507,35 +544,50 @@
 
     row16 = lax.broadcasted_iota(jnp.int32, (16, 128), 0)
     ahead = ct[0] - LAG + stream.n_slots
-
-    @pl.loop(0, N_GROUP)
-    def _(j):
-        slot = stream.wait(ct, j)
-        for r in range(GROUP):
-            seq = j * GROUP + r
-            spot = lax.rem(pos_s[seq], WINDOW)
-            base = pl.multiple_of(r * WINDOW + lax.div(spot, 16) * 16, 16)
-            for i, new in enumerate((k_new, v_new)):
-                here = (slot, pl.ds(base, 16), pl.ds(128 * i, 128))
-                slots[here] = jnp.where(row16 == lax.rem(spot, 16), new[pl.ds(seq, 1), :], f32(slots[here])).astype(BF)
-        for c in outputs(j):
-            c.start()
-        for r in range(GROUP):
-            seq = j * GROUP + r
-            q = q3[pl.ds(pl.multiple_of(seq * HEADS, HEADS), HEADS), :].astype(BF)
-            keys = slots[slot, r * WINDOW:(r + 1) * WINDOW, 0:128]
-            score = lax.dot_general(q, keys, (((1,), (1,)), ((), ())), preferred_element_type=F32) * (128 ** -0.5)
-            score = score + bias[pl.ds(seq, 1), :]
-            p = jnp.exp(score - jnp.max(score, axis=-1, keepdims=True))
-            p = (p / jnp.sum(p, axis=-1, keepdims=True)).astype(BF)
-            o = jnp.dot(p, slots[slot, r * WINDOW:(r + 1) * WINDOW, 128:256], preferred_element_type=F32)
-            o3[pl.ds(pl.multiple_of(seq * HEADS, HEADS), HEADS), :] = o
-
-        @pl.when(j >= LAG)
+    nt = (((1,), (1,)), ((), ()))
+
+    @pl.loop(0, N_GROUP // 2)
+    def _(p):
+        got = [stream.wait(ct, 2 * p + g) for g in range(2)]
+        for g, slot in enumerate(got):
+            for r in range(GROUP):
+                seq = (2 * p + g) * GROUP + r
+                spot = lax.rem(pos_s[seq], WINDOW)
+                base = pl.multiple_of(r * WINDOW + lax.div(spot, 16) * 16, 16)
+                for i, new in enumerate((k_new, v_new)):
+                    here = (slot, pl.ds(base, 16), pl.ds(128 * i, 128))
+                    slots[here] = jnp.where(row16 == lax.rem(spot, 16), new[pl.ds(seq, 1), :], f32(slots[here])).astype(BF)
+            start(outputs(2 * p + g))
+
+        pairs = [(slot, h) for slot in got for h in range(GROUP // 2)]
+        first = 2 * p * GROUP
+        scores = []
+        for i, (slot, h) in enumerate(pairs):
+            q = q3[pl.ds(pl.multiple_of((first + 2 * i) * HEADS, 2 * HEADS), 2 * HEADS), :].astype(BF)
+            halves = []
+            for e in range(2):
+                r = 2 * h + e
+                keys = slots[slot, r * WINDOW:(r + 1) * WINDOW, 0:128]
+                score = lax.dot_general(q, keys, nt, preferred_element_type=F32)[HEADS * e:HEADS * (e + 1)] * (128 ** -0.5)
+                halves.append(score + bias[pl.ds(first + 2 * i + e, 1), :])
+            scores.append(jnp.concatenate(halves, axis=0))
+        probs = []
+        for score in scores:
+            e = jnp.exp(score - jnp.max(score, axis=-1, keepdims=True))
+            probs.append((e / jnp.sum(e, axis=-1, keepdims=True)).astype(BF))
+        for i, (slot, h) in enumerate(pairs):
+            halves = []
+            for e in range(2):
+                r = 2 * h + e
+                values = slots[slot, r * WINDOW:(r + 1) * WINDOW, 128:256]
+                halves.append(jnp.dot(probs[i], values, preferred_element_type=F32)[HEADS * e:HEADS * (e + 1)])
+            o3[pl.ds(pl.multiple_of((first + 2 * i) * HEADS, 2 * HEADS), 2 * HEADS), :] = jnp.concatenate(halves, axis=0)
+
+        @pl.when(2 * p >= LAG)
         def _():
-            for c in outputs(j - LAG):
-                c.wait()
-            stream.issue(ahead + j, ahead + LAG, ahead + N_GROUP)
+            for g in range(2):
+                finish(outputs(2 * p + g - LAG))
+                stream.issue(ahead + 2 * p + g, ahead + LAG, ahead + N_GROUP)
 
     for h in range(HEADS):
         o_bf[:, 128 * h:128 * (h + 1)] = o3[pl.ds(h, ROWS, stride=HEADS), :].astype(BF)
@@ -551,22 +603,12 @@
     last = pltpu.make_async_copy(part, part_out, small_sem.at[0])
     last.start()
     for j in range(N_GROUP - LAG, N_GROUP):
-        for c in outputs(j):
-            c.wait()
-    slot_copy.wait()
+        finish(outputs(j))
+    finish(results)
     last.wait()
 
 
 ANY = pl.BlockSpec(memory_space=pl.ANY)
-
-
-def rope_tables(tok_pos):
-    quarter = 32
-    inv_freq = ROPE_BASE ** (-jnp.arange(quarter, dtype=F32) / quarter)
-    angles = tok_pos.astype(F32)[:, None] * inv_freq[None, :]
-    cosine, sine = jnp.cos(angles), jnp.sin(angles)
-    rows = tok_pos.shape[0]
-    return (jnp.concatenate([cosine, cosine, jnp.ones((rows, 64), F32)], axis=1), jnp.concatenate([-sine, sine, jnp.zeros((rows, 64), F32)], axis=1))
 
 
 def io_specs():
@@ -585,44 +627,43 @@
 
     def local_step(x_in, tok_pos, conv_state, lru_state, k_cache, v_cache, slot_pos, norm_scale, rec_wx, rec_bx, rec_wy, rec_by, conv_w, conv_b, gate_wa, gate_ba, gate_wi, gate_bi, a_param, rec_wout, rec_bout, attn_wq, attn_wk, attn_wv, attn_wo, attn_bo, mlp_w1, mlp_b1, mlp_w2, mlp_b2, mlp_wd, mlp_bd):
         tok = tok_pos.reshape(1, ROWS)
-        scales = norm_scale.reshape(6, D)
-        cosine, sine = rope_tables(tok_pos)
+        conv_t = jnp.transpose(conv_state, (0, 2, 1, 3))
         vec = pltpu.VMEM((2, 1408), BF)
-        x_mid, conv_out, lru_out = pl.pallas_call(
+        x_mid, xb, lru_mid = pl.pallas_call(
             recurrent_kernel,
-            out_shape=[shape((ROWS, D), BF), shape((2, 3, ROWS, 1408), BF), shape((2, ROWS, 1408), F32)],
+            out_shape=[shape((ROWS, D), BF), shape((2, ROWS, 1408), BF), shape((2, ROWS, 1408), F32)],
             in_specs=[ANY] * 24, out_specs=[ANY] * 3,
             scratch_shapes=body_scratch(N_SLOTS_A, 2) + [pltpu.VMEM((ROWS, 3072), BF), pltpu.VMEM((ROWS, 128), F32)] + COMM_SCRATCH + [
-                pltpu.VMEM((1, ROWS), jnp.int32), pltpu.VMEM((6, D), BF), vec, vec, pltpu.VMEM((2, 4, 1408), BF), vec, vec, vec, pltpu.VMEM((2, 1408), F32),
+                pltpu.VMEM((1, ROWS), jnp.int32), pltpu.VMEM((3, 2, D), BF), vec, vec, pltpu.VMEM((2, 4, 1408), BF), vec, vec, vec, pltpu.VMEM((2, 1408), F32),
                 pltpu.VMEM((2, D), BF), pltpu.VMEM((3, 3072), BF), pltpu.VMEM((3, 3072), BF), pltpu.VMEM((3, D), BF), pltpu.SemaphoreType.DMA((14,)),
                 pltpu.VMEM((2, 3, ROWS, 1408), BF), pltpu.VMEM((2, ROWS, 1408), F32), pltpu.VMEM((2, 8, 176, 176), BF), pltpu.VMEM((2, 8, 176, 176), BF),
-                pltpu.VMEM((ROWS, 1408), BF), pltpu.VMEM((ROWS, 1408), F32), pltpu.VMEM((ROWS, 1408), BF), pltpu.VMEM((ROWS, 1408), F32), pltpu.VMEM((ROWS, 1408), F32),
+                pltpu.VMEM((2, ROWS, 1408), BF), pltpu.VMEM((ROWS, 128), F32), pltpu.VMEM((ROWS, 1408), BF), pltpu.VMEM((ROWS, 1408), F32), pltpu.VMEM((ROWS, 1408), F32),
                 pltpu.VMEM((ROWS, 1408), BF), pltpu.VMEM((ROWS, 128), jnp.int32), pltpu.SemaphoreType.DMA((2, 4)), pltpu.SemaphoreType.DMA((2, 3))],
             compiler_params=pltpu.CompilerParams(collective_id=0, has_side_effects=True, vmem_limit_bytes=VMEM_LIMIT),
             name='recurrent_layers',
-        )(tok, x_in, jnp.transpose(conv_state, (0, 2, 1, 3)), lru_state, scales, rec_wx, rec_bx, rec_wy, rec_by, conv_w, conv_b, gate_wa, gate_ba, gate_wi, gate_bi, a_param, rec_wout, rec_bout, mlp_w1, mlp_b1, mlp_w2, mlp_b2, mlp_wd, mlp_bd)
+        )(tok, x_in, conv_t, lru_state, norm_scale, rec_wx, rec_bx, rec_wy, rec_by, conv_w, conv_b, gate_wa, gate_ba, gate_wi, gate_bi, a_param, rec_wout, rec_bout, mlp_w1, mlp_b1, mlp_w2, mlp_b2, mlp_wd, mlp_bd)
         cache = (ROWS * WINDOW, 128)
         table = pltpu.VMEM((ROWS, 128), F32)
-        part, k_out, v_out, slot_out = pl.pallas_call(
+        part, conv_out, lru_out, k_out, v_out, slot_out = pl.pallas_call(
             attention_kernel,
-            out_shape=[shape((N_CHUNK, 2, HALF, CHUNK), BF), shape(cache, BF), shape(cache, BF), shape((ROWS, WINDOW), jnp.int32)],
-            in_specs=[pl.BlockSpec(memory_space=pltpu.SMEM)] + [ANY] * 12, out_specs=[ANY] * 4,
+            out_shape=[shape((N_CHUNK, 2, HALF, CHUNK), BF), shape((2, 3, ROWS, 1408), BF), shape((2, ROWS, 1408), F32), shape(cache, BF), shape(cache, BF), shape((ROWS, WINDOW), jnp.int32)],
+            in_specs=[pl.BlockSpec(memory_space=pltpu.SMEM)] + [ANY] * 14, out_specs=[ANY] * 6,
             scratch_shapes=body_scratch(N_SLOTS_B, 4) + [
-                table, pltpu.VMEM((6, D), BF), pltpu.VMEM((1, ROWS), jnp.int32), table, table, pltpu.VMEM((ROWS, WINDOW), jnp.int32), pltpu.VMEM((ROWS, WINDOW), F32),
+                table, pltpu.VMEM((3, 2, D), BF), pltpu.VMEM((1, ROWS), jnp.int32), pltpu.VMEM((1, 128), F32), table, table, pltpu.VMEM((2, 3, ROWS, 1408), BF), pltpu.VMEM((2, ROWS, 1408), F32), pltpu.VMEM((ROWS, WINDOW), jnp.int32), pltpu.VMEM((ROWS, WINDOW), F32),
                 pltpu.VMEM((ROWS, 128), jnp.int32), pltpu.VMEM((ROWS * HEADS, 128), F32), pltpu.VMEM((ROWS * HEADS, 128), F32), table, table,
-                pltpu.VMEM((ROWS, 1024), BF), pltpu.VMEM((N_CHUNK, 2, HALF, CHUNK), BF), pltpu.SemaphoreType.DMA((6,)), pltpu.SemaphoreType.DMA((N_SLOTS_B, 2)), pltpu.SemaphoreType.DMA],
+                pltpu.VMEM((ROWS, 1024), BF), pltpu.VMEM((N_CHUNK, 2, HALF, CHUNK), BF), pltpu.SemaphoreType.DMA((5,)), pltpu.SemaphoreType.DMA((3,)), pltpu.SemaphoreType.DMA((N_SLOTS_B, 2))],
             compiler_params=pltpu.CompilerParams(vmem_limit_bytes=VMEM_LIMIT),
             name='attention_layer',
-        )(tok_pos, tok, x_mid, scales, cosine, sine, k_cache.reshape(cache), v_cache.reshape(cache), slot_pos, attn_wq, attn_wk, attn_wv, attn_wo)
+        )(tok_pos, tok, x_mid, norm_scale, jnp.asarray(FREQ), conv_t, xb, lru_mid, k_cache.reshape(cache), v_cache.reshape(cache), slot_pos, attn_wq, attn_wk, attn_wv, attn_wo)
         x_out = pl.pallas_call(
             final_kernel,
             out_shape=shape((ROWS, D), BF),
-            in_specs=[ANY] * 10, out_specs=ANY,
-            scratch_shapes=body_scratch(N_SLOTS_C, 1) + [pltpu.VMEM((ROWS, 3072), BF), pltpu.VMEM((ROWS, 128), F32)] + COMM_SCRATCH + [
-                pltpu.VMEM((6, D), BF), pltpu.VMEM((1, D), BF), pltpu.VMEM((3, 3072), BF), pltpu.VMEM((3, 3072), BF), pltpu.VMEM((3, D), BF), pltpu.SemaphoreType.DMA((7,))],
+            in_specs=[ANY] * 10, out_specs=pl.BlockSpec(memory_space=pltpu.VMEM),
+            scratch_shapes=body_scratch(N_SLOTS_C, 1)[:3] + [pltpu.VMEM((ROWS, 3072), BF), pltpu.VMEM((ROWS, 128), F32)] + COMM_SCRATCH + [
+                pltpu.VMEM((3, 2, D), BF), pltpu.VMEM((D,), BF), pltpu.VMEM((3, 3072), BF), pltpu.VMEM((3, 3072), BF), pltpu.VMEM((3, D), BF), pltpu.SemaphoreType.DMA((7,))],
             compiler_params=pltpu.CompilerParams(collective_id=1, has_side_effects=True, vmem_limit_bytes=VMEM_LIMIT),
             name='last_mlp',
-        )(x_mid, part, scales, attn_bo.reshape(1, D), mlp_w1, mlp_b1, mlp_w2, mlp_b2, mlp_wd, mlp_bd)
+        )(x_mid, part, norm_scale, attn_bo, mlp_w1, mlp_b1, mlp_w2, mlp_b2, mlp_wd, mlp_bd)
         return (x_out, jnp.transpose(conv_out, (0, 2, 1, 3)), lru_out, k_out.reshape(k_cache.shape), v_out.reshape(v_cache.shape), slot_out)
 
     return jax.shard_map(local_step, mesh=mesh, in_specs=in_specs, out_specs=out_specs, check_vma=False)

time: 237 us -> 214 us (0.903)
  Pallas kernels: 223 us -> 211 us
  local copies, waits for them, and re-layouts: 10.9 us -> 2.29 us
    pallas_call x1, Pallas kernels: 64.6 us -> 54.4 us  [local_step(): pl.pallas_call(attention_kernel, out_shape=[shape((N_CHUNK, 2, HALF, CHUN...]
    unnamed x3 -> x1, local copies, waits for them, and re-layouts: 7.95 us -> 2.29 us
    reshape x2 -> x0, local copies, waits for them, and re-layouts: 2.76 us -> none  [the longest x1 1.45 us: local_step(): scales = norm_scale.reshape(6, D)]
where the time goes in v2:
time: 214 us
  Pallas kernels  211 us (99%)
  local copies, waits for them, and re-layouts  2.29 us (1%)
    pallas_call x1, Pallas kernels, local_step(): pl.pallas_call(recurrent_kernel, out_shape=[shape((ROWS, D), BF), shape((...  110 us
    pallas_call x1, Pallas kernels, local_step(): pl.pallas_call(attention_kernel, out_shape=[shape((N_CHUNK, 2, HALF, CHUN...  54.4 us
    pallas_call x1, Pallas kernels, local_step(): pl.pallas_call(final_kernel, out_shape=shape((ROWS, D), BF), in_specs=[AN...  46.5 us

profile of v2, /device:TPU:0, one launch (start us, length us, event | category | flops | bytes accessed | tf_op | source)
XLA Modules:
  0.0 214.1 jit_solution(15431371385442615892)
XLA Ops:
  0.6 110.3 %recurrent_layers.1 = (bf16[128,4096]{1,0:T(8,128)(2,1)}, bf16[2,128,1408]{2,1,0:T(8,128)(2,1)}, f32[2,128,1408]{2,1,0:T(8,128)}) custom-call(s32[1,128]{1,0:T(1,128)} %bitcast.11, bf16[128,4096]{1,0:T(8,128)(2,1)} %x_in.1, bf16[2,3,128,1408]{3,2,1,0:T(8,128)(2,1)} %bitcast.9, f32[2,128,1408]{2,1,0:T(8,128)} %lru.1, bf16[3,2,4096]{2,1,0:T(2,128)(2,1)} %nscale.5, ...), custom_call_target="tpu_custom_call" | custom-call | tf_op jit(solution)/shard_map/recurrent_layers/pallas_call | solution.py:632
  111.0 54.4 %attention_layer.1 = (bf16[8,2,64,512]{3,2,1,0:T(8,128)(2,1)}, bf16[2,3,128,1408]{3,2,1,0:T(8,128)(2,1)}, f32[2,128,1408]{2,1,0:T(8,128)}, bf16[131072,128]{1,0:...) custom-call(s32[128]{0:T(128)} %pos_s.1, s32[1,128]{1,0:T(1,128)} %bitcast.12, ...), custom_call_target="tpu_custom_call" | custom-call | tf_op jit(solution)/shard_map/attention_layer/pallas_call | solution.py:647
  165.3 46.5 %last_mlp.1 = bf16[128,4096]{1,0:T(8,128)(2,1)} custom-call(bf16[128,4096]{1,0:T(8,128)(2,1)} %get-tuple-element.15.x_in, bf16[8,2,64,512]{3,2,1,0:T(8,128)(2,1)} %get-tuple-element.18.part_in, bf16[3,2,4096]{2,1,0:T(2,128)(2,1)} %nscale.5, bf16[4096]{0:T(1024)(128)(2,1)} %bo.1, bf16[3,4096,3072]{2,1,0:T(8,128)(2,1)} %w1.3, bf16[3,3072]{1,0:T(4,128)(2,1)} %b1.3, ...), custom_call_target="tpu_custom_call" | custom-call | tf_op jit(solution)/shard_map/last_mlp/pallas_call | solution.py:658
  211.8 2.3 %copy.40 = bf16[128,4096]{1,0:T(8,128)(2,1)} copy(bf16[128,4096]{1,0:T(8,128)(2,1)} %last_mlp.1) | data formatting | bytes 2097152

commit v3 on v2

--- a/solution.py
+++ b/solution.py
@@ -11,6 +11,7 @@
 BF = jnp.bfloat16
 F32 = jnp.float32
 ROWS = 128
+LOCAL = 1408
 D = 4096
 TILE = 256
 CHUNK = 512
@@ -62,12 +63,11 @@
             else:
                 pl.when(jnp.logical_and(t >= start, t < start + n))(go)
 
-    def prime(self):
-        first = min(self.n_slots, self.total)
+    def prime(self, lo, hi):
         for start, n, kinds in self.phases:
-            stop = min(start + n, first)
-            if start < stop:
-                @pl.loop(start, stop)
+            first, stop = max(start, lo), min(start + n, hi, self.n_slots)
+            if first < stop:
+                @pl.loop(first, stop)
                 def _(t, start=start, kinds=kinds):
                     self.start_tile(kinds, t - start, self.slot_of(t))
 
@@ -229,17 +229,17 @@
         ahead = start + st.n_slots
         stop = ahead + 24
 
-        @pl.loop(0, 12)
-        def _(i):
-            s0 = st.wait(up, 2 * i)
-            s1 = st.wait(up, 2 * i + 1)
-            g = jnp.dot(self.n[...], st.slots[s0], preferred_element_type=F32)
-            v = jnp.dot(self.n[...], st.slots[s1], preferred_element_type=F32)
-            st.issue(ahead + 2 * i, ahead, stop)
-            st.issue(ahead + 2 * i + 1, ahead, stop)
-            g = g + f32(b1[layer:layer + 1, cols(i, TILE)])
-            v = v + f32(b2[layer:layer + 1, cols(i, TILE)])
-            self.hid[:, cols(i, TILE)] = (gelu(g) * v).astype(BF)
+        @pl.loop(0, 6)
+        def _(q):
+            got = [st.wait(up, 4 * q + h) for h in range(4)]
+            dots = [jnp.dot(self.n[...], st.slots[slot], preferred_element_type=F32) for slot in got]
+            for h in range(4):
+                st.issue(ahead + 4 * q + h, ahead, stop)
+            for h in range(2):
+                c = cols(2 * q + h, TILE)
+                gate = dots[2 * h] + f32(b1[layer:layer + 1, c])
+                lin = dots[2 * h + 1] + f32(b2[layer:layer + 1, c])
+                self.hid[:, c] = (gelu(gate) * lin).astype(BF)
 
         self.down(down, 3072, 2, self.hid)
         self.all_reduce(bd, layer)
@@ -255,7 +255,7 @@
             return [jnp.dot(self.n[...], st.slots[slot], preferred_element_type=F32) for slot in slots]
 
         def put_x(i, g):
-            v.xb[layer, :, cols(i, TILE)] = (g + f32(v.bx[layer:layer + 1, cols(i, TILE)])).astype(BF)
+            v.xb[:, cols(i, TILE)] = (g + f32(v.bx[layer:layer + 1, cols(i, TILE)])).astype(BF)
 
         @pl.loop(0, 2)
         def _(p):
@@ -271,7 +271,7 @@
         for h in range(2):
             st.issue(ahead + 4 + h, ahead, stop)
         put_x(4, last_x)
-        v.xb[layer, :, 1280:1408] = (g[:, 0:128] + f32(v.bx[layer:layer + 1, 1280:1408])).astype(BF)
+        v.xb[:, 1280:1408] = (g[:, 0:128] + f32(v.bx[layer:layer + 1, 1280:1408])).astype(BF)
         v.yg[...] = gelu(g[:, 128:256] + f32(v.by[layer:layer + 1, 1280:1408]))
 
         outs.wait_inputs(layer)
@@ -280,16 +280,16 @@
         @pl.loop(0, 11)
         def _(i):
             c = cols(i, 128)
-            acc = f32(v.cb[layer:layer + 1, c]) + f32(v.cw[layer, 0:1, c]) * f32(v.xb[layer, :, c])
+            acc = f32(v.cb[layer:layer + 1, c]) + f32(v.cw[layer, 0:1, c]) * f32(v.xb[:, c])
             for j in range(3):
-                acc = acc + jnp.where(pos >= 3 - j, f32(v.conv[layer, j, :, c]), 0.0) * f32(v.cw[layer, 3 - j:4 - j, c])
+                acc = acc + jnp.where(pos >= 3 - j, f32(v.conv[j, :, c]), 0.0) * f32(v.cw[layer, 3 - j:4 - j, c])
             v.xc[:, c] = acc.astype(BF)
 
         for b in range(8):
             c = slice(176 * b, 176 * (b + 1))
             xc = v.xc[:, c]
-            v.rp[:, c] = jnp.dot(xc, v.ga[layer, b], preferred_element_type=F32)
-            v.ip[:, c] = jnp.dot(xc, v.gi[layer, b], preferred_element_type=F32)
+            v.rp[:, c] = jnp.dot(xc, v.ga[b], preferred_element_type=F32)
+            v.ip[:, c] = jnp.dot(xc, v.gi[b], preferred_element_type=F32)
 
         def gate(c, reset):
             rate = -8.0 * jax.nn.softplus(v.ap[layer:layer + 1, c])
@@ -297,8 +297,8 @@
             into = jnp.sqrt(1.0 - decay * decay)
             decay = jnp.where(reset, 0.0, decay)
             into = jnp.where(reset, 1.0, into)
-            new = decay * v.lru[layer, :, c] + into * jax.nn.sigmoid(v.ip[:, c] + f32(v.gbi[layer:layer + 1, c])) * f32(v.xc[:, c])
-            v.lru[layer, :, c] = new
+            new = decay * v.lru[:, c] + into * jax.nn.sigmoid(v.ip[:, c] + f32(v.gbi[layer:layer + 1, c])) * f32(v.xc[:, c])
+            v.lru[:, c] = new
             return new
 
         def put_y(i, g):
@@ -324,6 +324,8 @@
         self.down(out_tiles, 1408, 1, v.gated)
         self.all_reduce(v.bout, layer)
         outs.wait_write(layer)
+        if layer == 0:
+            outs.start_inputs(1)
 
 
 def add_mlp(stream, w1, w2, wd, layer):
@@ -341,7 +343,7 @@
         self.ins, self.xb_out, self.lru_out, self.v, self.in_sem, self.out_sem = ins, xb_out, lru_out, v, in_sem, out_sem
 
     def inputs(self, layer):
-        return [pltpu.make_async_copy(src.at[layer], dst.at[layer], self.in_sem.at[layer, i]) for i, (src, dst) in enumerate(self.ins)]
+        return [pltpu.make_async_copy(src.at[layer], dst, self.in_sem.at[layer, i]) for i, (src, dst) in enumerate(self.ins)]
 
     def start_inputs(self, layer):
         for c in self.inputs(layer):
@@ -352,7 +354,7 @@
             c.wait()
 
     def outputs(self, layer):
-        pairs = [(self.v.xb.at[layer], self.xb_out.at[layer]), (self.v.lru.at[layer], self.lru_out.at[layer])]
+        pairs = [(self.v.xb, self.xb_out.at[layer]), (self.v.lru, self.lru_out.at[layer])]
         return [pltpu.make_async_copy(src, dst, self.out_sem.at[layer, i]) for i, (src, dst) in enumerate(pairs)]
 
     def write(self, layer):
@@ -364,9 +366,33 @@
             c.wait()
 
 
-N_SLOTS_A = 20
+N_SLOTS_A = 19
+WINDOW = 1024
+HEADS = 8
+N_COMM = 12
+N_SMALL = 15
+LEFT = pl.ds(0, 128)
+RIGHT = pl.ds(128, 128)
+FREQ = np.zeros((1, 128), np.float32)
+FREQ[0, :32] = FREQ[0, 32:64] = np.float32(ROPE_BASE) ** (-np.arange(32, dtype=np.float32) / 32)
+
+
+def copies(pairs, sem):
+    return [pltpu.make_async_copy(a, b, sem.at[i]) for i, (a, b) in enumerate(pairs)]
+
+
+def start(group):
+    for c in group:
+        c.start()
+
+
+def finish(group):
+    for c in group:
+        c.wait()
+
+
 N_SLOTS_B = 22
-N_SLOTS_C = 24
+N_SLOTS_C = 23
 
 COMM_SCRATCH = [
     pltpu.VMEM((N_CHUNK, 2, HALF, CHUNK), BF), pltpu.VMEM((N_CHUNK, HALF, CHUNK), BF), pltpu.VMEM((N_CHUNK, HALF, CHUNK), BF),
@@ -378,13 +404,14 @@
     return [pltpu.VMEM((n_slots, D, TILE), BF), pltpu.SemaphoreType.DMA((n_slots, n_pieces)), pltpu.VMEM((ROWS, D), BF), pltpu.VMEM((ROWS, D), BF)]
 
 
-def recurrent_kernel(tok, x_in, conv, lru, nscale, wx, bx, wy, by, cw, cb, ga, gba, gi, gbi, ap, wout, bout, w1, b1, w2, b2, wd, bd, *refs):
-    x_out, xb_out, lru_out = refs[:3]
-    slots, sems, x, n, hid, ss = refs[3:9]
-    comm = Comm(*refs[9:21])
-    small = refs[21:35]
-    v_tok, v_ns, v_bx, v_by, v_cw, v_cb, v_gba, v_gbi, v_ap, v_bout, v_b1, v_b2, v_bd, small_sem = small
-    v_conv, v_lru, v_ga, v_gi, xb, yg, xc, rp, ip, gated, tokc, in_sem, out_sem = refs[35:]
+def recurrent_kernel(tok, x_in, conv, lru, nscale, wx, bx, wy, by, cw, cb, ga, gba, gi, gbi, ap, wout, bout, w1, b1, w2, b2, wd, bd, freq, wq, wk, wv, *refs):
+    (x_out, xb_out, lru_out, q_out, k_row, v_row), refs = refs[:6], refs[6:]
+    (slots, sems, x, n, hid, ss), refs = refs[:6], refs[6:]
+    comm = Comm(*refs[:N_COMM])
+    refs = refs[N_COMM:]
+    small, refs = refs[:N_SMALL], refs[N_SMALL:]
+    v_tok, v_ns, v_bx, v_by, v_cw, v_cb, v_gba, v_gbi, v_ap, v_bout, v_b1, v_b2, v_bd, v_freq, small_sem = small
+    v_conv, v_lru, v_ga, v_gi, xb, yg, xc, rp, ip, gated, tokc, q3, k_new, v_new, v_cos, v_sin, in_sem, out_sem, row_sem = refs
     stream = Stream(slots, sems, N_SLOTS_A)
     v = Names(bx=v_bx, by=v_by, cw=v_cw, cb=v_cb, ga=v_ga, gba=v_gba, gi=v_gi, gbi=v_gbi, ap=v_ap, bout=v_bout, conv=v_conv, lru=v_lru, xb=xb, yg=yg, xc=xc, rp=rp, ip=ip, gated=gated, tokc=tokc)
     outs = StateCopies([(conv, v_conv), (lru, v_lru), (ga, v_ga), (gi, v_gi)], xb_out, lru_out, v, in_sem, out_sem)
@@ -398,15 +425,16 @@
         ot = stream.add(8, lambda j, layer=layer: [(wout.at[layer, :, pl.ds(pl.multiple_of(j * CHUNK + h * TILE, TILE), TILE)], (pl.ds(h * 1408, 1408), pl.ds(0, TILE))) for h in range(2)])
         up, down = add_mlp(stream, w1, w2, wd, layer)
         plan.append((xt, mixed, yt, ot, up, down))
-
-    pairs = [(x_in, x), (tok, v_tok), (nscale, v_ns), (bx, v_bx), (by, v_by), (cw, v_cw), (cb, v_cb), (gba, v_gba), (gbi, v_gbi), (ap, v_ap), (bout, v_bout), (b1, v_b1), (b2, v_b2), (bd, v_bd)]
-    early = [pltpu.make_async_copy(s, d, small_sem.at[i]) for i, (s, d) in enumerate(pairs)]
-    for c in early:
-        c.start()
+    qt = stream.add(4, lambda j: [(wq.at[:, cols(j, TILE)], full(D))])
+    kvt = stream.add(1, lambda j: [(wk, (pl.ds(0, D), LEFT)), (wv, (pl.ds(0, D), RIGHT))])
+
+    pairs = [(x_in, x), (tok, v_tok), (nscale, v_ns), (bx, v_bx), (by, v_by), (cw, v_cw), (cb, v_cb), (gba, v_gba), (gbi, v_gbi), (ap, v_ap), (bout, v_bout), (b1, v_b1), (b2, v_b2), (bd, v_bd), (freq, v_freq)]
+    early = copies(pairs, small_sem)
+    start(early)
     comm.greet()
-    stream.prime()
+    stream.prime(0, 6)
     outs.start_inputs(0)
-    outs.start_inputs(1)
+    stream.prime(6, N_SLOTS_A)
     for c in early:
         c.wait()
     tokc[...] = jnp.broadcast_to(v_tok[...], (ROWS, 128)).T
@@ -419,36 +447,51 @@
         body.mlp(up, down, layer, v_b1, v_b2, v_bd)
     last = pltpu.make_async_copy(x, x_out, small_sem.at[0])
     last.start()
+    body.norm(4)
+    lane = lax.broadcasted_iota(jnp.int32, (ROWS, 128), 1)
+    angle = f32(tokc[...]) * v_freq[...]
+    v_cos[...] = jnp.cos(angle)
+    v_sin[...] = jnp.sin(angle) * jnp.where(lane < 32, -1.0, 1.0)
+
+    def rope(val):
+        other = jnp.where(lane < 32, pltpu.roll(val, 96, 1), pltpu.roll(val, 32, 1))
+        return f32((val * v_cos[...] + other * v_sin[...]).astype(BF))
+
+    @pl.loop(0, 2)
+    def _(p):
+        got = [stream.wait(qt, 2 * p + i) for i in range(2)]
+        for i, slot in enumerate(got):
+            g = jnp.dot(n[...], slots[slot], preferred_element_type=F32)
+            for h in range(2):
+                q3[pl.ds(4 * p + 2 * i + h, ROWS, stride=HEADS), :] = rope(g[:, 128 * h:128 * (h + 1)])
+
+    slot = stream.wait(kvt, 0)
+    g = jnp.dot(n[...], slots[slot], preferred_element_type=F32)
+    k_new[...] = rope(g[:, :128])
+    v_new[...] = f32(g[:, 128:].astype(BF))
+    rows = copies([(q3, q_out), (k_new, k_row), (v_new, v_row)], row_sem)
+    start(rows)
+    finish(rows)
     last.wait()
 
 
-def final_kernel(x_in, part_in, nscale, bo, w1, b1, w2, b2, wd, bd, *refs):
-    x, slots, sems, n, hid, ss = refs[:6]
-    comm = Comm(*refs[6:18])
-    v_ns, v_bo, v_b1, v_b2, v_bd, small_sem = refs[18:]
+def final_kernel(x_in, o_in, nscale, bo, wo, w1, b1, w2, b2, wd, bd, *refs):
+    (x, slots, sems, n, hid, ss), refs = refs[:6], refs[6:]
+    comm = Comm(*refs[:N_COMM])
+    v_ns, v_bo, v_b1, v_b2, v_bd, o3, o_bf, small_sem = refs[N_COMM:]
     stream = Stream(slots, sems, N_SLOTS_C)
     body = Body(stream, comm, x, n, hid, ss, v_ns)
+    ot = stream.add(8, lambda j: [(wo.at[:, pl.ds(pl.multiple_of(j * CHUNK + h * TILE, TILE), TILE)], (pl.ds(h * WINDOW, WINDOW), pl.ds(0, TILE))) for h in range(2)])
     up, down = add_mlp(stream, w1, w2, wd, 2)
-    pairs = [(part_in, comm.part), (x_in, x), (nscale, v_ns), (bo, v_bo), (b1, v_b1), (b2, v_b2), (bd, v_bd)]
-    early = [pltpu.make_async_copy(s, d, small_sem.at[i]) for i, (s, d) in enumerate(pairs)]
-    for c in early:
-        c.start()
+    early = copies([(o_in, o3), (x_in, x), (nscale, v_ns), (bo, v_bo), (b1, v_b1), (b2, v_b2), (bd, v_bd)], small_sem)
+    start(early)
     comm.greet()
-    stream.prime()
-    early[0].wait()
+    stream.prime(0, N_SLOTS_C)
+    finish(early)
+    for h in range(HEADS):
+        o_bf[:, 128 * h:128 * (h + 1)] = o3[pl.ds(h, ROWS, stride=HEADS), :].astype(BF)
     comm.meet()
-
-    @pl.loop(0, N_CHUNK)
-    def _(k):
-        comm.copy1(0, k).start()
-
-    for c in early[1:]:
-        c.wait()
-
-    @pl.loop(0, N_CHUNK)
-    def _(k):
-        comm.chip_sum(0, k)
-
+    body.down(ot, WINDOW, 1, o_bf)
     body.all_reduce(v_bo, None)
     body.norm(5)
     body.mlp(up, down, 2, v_b1, v_b2, v_bd)
@@ -456,53 +499,27 @@
 
 GROUP = 4
 N_GROUP = ROWS // GROUP
-WINDOW = 1024
-HEADS = 8
 LAG = 4
-FREQ = np.zeros((1, 128), np.float32)
-FREQ[0, :32] = FREQ[0, 32:64] = np.float32(ROPE_BASE) ** (-np.arange(32, dtype=np.float32) / 32)
-
-
-def attention_kernel(pos_s, tok, x_in, nscale, freq, conv, xb, lru, k_cache, v_cache, slot_pos, wq, wk, wv, wo, part_out, conv_out, lru_out, k_out, v_out, slot_out,
-                     slots, sems, x, n, ss, v_ns, v_tok, v_freq, v_cos, v_sin, v_conv, v_lru, v_slot, bias, tokc, q3, o3, k_new, v_new, o_bf, part, small_sem, state_sem, out_sem):
+
+
+def attention_kernel(pos_s, tok, q_in, k_row, v_row, conv, xb, lru, k_cache, v_cache, slot_pos, o_out, conv_out, lru_out, k_out, v_out, slot_out,
+                     slots, sems, v_tok, v_conv, v_lru, v_slot, bias, q3, o3, k_new, v_new, small_sem, state_sem, out_sem):
     stream = Stream(slots, sems, N_SLOTS_B)
-    body = Body(stream, None, x, n, None, ss, v_ns)
-    qt = stream.add(4, lambda j: [(wq.at[:, cols(j, TILE)], full(D))])
-    kvt = stream.add(1, lambda j: [(wk, (pl.ds(0, D), pl.ds(0, 128))), (wv, (pl.ds(0, D), pl.ds(128, 128)))])
 
     def group_rows(j):
         return pl.ds(pl.multiple_of(j * GROUP * WINDOW, GROUP * WINDOW), GROUP * WINDOW)
 
-    ct = stream.add(N_GROUP, lambda j: [(src.at[group_rows(j)], (pl.ds(0, D), pl.ds(128 * i, 128))) for i, src in enumerate((k_cache, v_cache))])
-    ot = stream.add(4, lambda j: [(wo.at[:, cols(4 * j + h, TILE)], (pl.ds(1024 * h, 1024), pl.ds(0, TILE))) for h in range(4)])
-
-    def copies(pairs, sem):
-        return [pltpu.make_async_copy(a, b, sem.at[i]) for i, (a, b) in enumerate(pairs)]
-
-    def start(group):
-        for c in group:
-            c.start()
-
-    def finish(group):
-        for c in group:
-            c.wait()
-
-    early = copies([(x_in, x), (tok, v_tok), (nscale, v_ns), (freq, v_freq), (slot_pos, v_slot)], small_sem)
+    ct = stream.add(N_GROUP, lambda j: [(src.at[group_rows(j)], (pl.ds(0, D), part)) for part, src in ((LEFT, k_cache), (RIGHT, v_cache))])
+    early = copies([(tok, v_tok), (slot_pos, v_slot), (q_in, q3), (k_row, k_new), (v_row, v_new)], small_sem)
     start(early)
-    stream.prime()
+    stream.prime(0, N_SLOTS_B // 2)
     states = copies([(conv.at[:, 1:3], v_conv.at[:, 0:2]), (xb, v_conv.at[:, 2]), (lru, v_lru)], state_sem)
     start(states)
+    stream.prime(N_SLOTS_B // 2, N_SLOTS_B)
     finish(early)
-    tokc[...] = jnp.broadcast_to(v_tok[...], (ROWS, 128)).T
-    body.squares()
-    body.norm(4)
-
-    pos = tokc[...]
+    pos = jnp.broadcast_to(v_tok[...], (ROWS, 128)).T
     target = lax.rem(pos, WINDOW)
     lane = lax.broadcasted_iota(jnp.int32, (ROWS, 128), 1)
-    angle = f32(pos) * v_freq[...]
-    v_cos[...] = jnp.cos(angle)
-    v_sin[...] = jnp.sin(angle) * jnp.where(lane < 32, -1.0, 1.0)
 
     @pl.loop(0, WINDOW // 128)
     def _(i):
@@ -512,31 +529,7 @@
         good = (now >= 0) & (age >= 0) & (age < WINDOW)
         bias[:, cols(i, 128)] = jnp.where(good, 0.0, -jnp.inf)
 
-    def rope(val):
-        other = jnp.where(lane < 32, pltpu.roll(val, 96, 1), pltpu.roll(val, 32, 1))
-        return val * v_cos[...] + other * v_sin[...]
-
-    ahead = stream.n_slots
-
-    @pl.loop(0, 2)
-    def _(p):
-        got = [stream.wait(qt, 2 * p + i) for i in range(2)]
-        for i, slot in enumerate(got):
-            g = jnp.dot(n[...], slots[slot], preferred_element_type=F32)
-            for h in range(2):
-                q3[pl.ds(4 * p + 2 * i + h, ROWS, stride=HEADS), :] = f32(rope(g[:, 128 * h:128 * (h + 1)]).astype(BF))
-        for i in range(2):
-            stream.issue(ahead + 2 * p + i, ahead, ahead + 4)
-
-    slot = stream.wait(kvt, 0)
-    g = jnp.dot(n[...], slots[slot], preferred_element_type=F32)
-    stream.issue(ahead + 4, ahead + 4, ahead + 5)
-    k_new[...] = f32(rope(g[:, 0:128]).astype(BF))
-    v_new[...] = f32(g[:, 128:256].astype(BF))
-
-    finish(states)
     results = copies([(v_conv, conv_out), (v_lru, lru_out), (v_slot, slot_out)], state_sem)
-    start(results)
 
     def outputs(j):
         slot = stream.slot_of(ct[0] + j)
@@ -585,22 +578,16 @@
 
         @pl.when(2 * p >= LAG)
         def _():
+            @pl.when(2 * p == LAG)
+            def _():
+                finish(states)
+                start(results)
+
             for g in range(2):
                 finish(outputs(2 * p + g - LAG))
                 stream.issue(ahead + 2 * p + g, ahead + LAG, ahead + N_GROUP)
 
-    for h in range(HEADS):
-        o_bf[:, 128 * h:128 * (h + 1)] = o3[pl.ds(h, ROWS, stride=HEADS), :].astype(BF)
-
-    @pl.loop(0, 4)
-    def _(j):
-        slot = stream.wait(ot, j)
-        for h in range(4):
-            prod = jnp.dot(o_bf[...], slots[slot, 1024 * h:1024 * (h + 1), :], preferred_element_type=F32).astype(BF)
-            for r in range(2):
-                part[2 * j + h // 2, r, :, (h % 2) * TILE:(h % 2 + 1) * TILE] = prod[r * HALF:(r + 1) * HALF]
-
-    last = pltpu.make_async_copy(part, part_out, small_sem.at[0])
+    last = pltpu.make_async_copy(o3, o_out, small_sem.at[0])
     last.start()
     for j in range(N_GROUP - LAG, N_GROUP):
         finish(outputs(j))
@@ -628,42 +615,43 @@
     def local_step(x_in, tok_pos, conv_state, lru_state, k_cache, v_cache, slot_pos, norm_scale, rec_wx, rec_bx, rec_wy, rec_by, conv_w, conv_b, gate_wa, gate_ba, gate_wi, gate_bi, a_param, rec_wout, rec_bout, attn_wq, attn_wk, attn_wv, attn_wo, attn_bo, mlp_w1, mlp_b1, mlp_w2, mlp_b2, mlp_wd, mlp_bd):
         tok = tok_pos.reshape(1, ROWS)
         conv_t = jnp.transpose(conv_state, (0, 2, 1, 3))
-        vec = pltpu.VMEM((2, 1408), BF)
-        x_mid, xb, lru_mid = pl.pallas_call(
+        vec, vec_f = pltpu.VMEM((2, LOCAL), BF), pltpu.VMEM((2, LOCAL), F32)
+        wide, wide_f = pltpu.VMEM((ROWS, LOCAL), BF), pltpu.VMEM((ROWS, LOCAL), F32)
+        table, gates, heads = pltpu.VMEM((ROWS, 128), F32), pltpu.VMEM((8, 176, 176), BF), pltpu.VMEM((ROWS * HEADS, 128), F32)
+        scale, mlp_b, pos_row, freq = pltpu.VMEM((3, 2, D), BF), pltpu.VMEM((3, 3072), BF), pltpu.VMEM((1, ROWS), jnp.int32), jnp.asarray(FREQ)
+        hidden, out_b = pltpu.VMEM((ROWS, 3072), BF), pltpu.VMEM((3, D), BF)
+        dma = pltpu.SemaphoreType.DMA
+        row, head_rows, branch, state = shape((ROWS, 128), F32), shape((ROWS * HEADS, 128), F32), shape((2, ROWS, LOCAL), BF), shape((2, ROWS, LOCAL), F32)
+        x_mid, xb, lru_mid, q_rows, k_row, v_row = pl.pallas_call(
             recurrent_kernel,
-            out_shape=[shape((ROWS, D), BF), shape((2, ROWS, 1408), BF), shape((2, ROWS, 1408), F32)],
-            in_specs=[ANY] * 24, out_specs=[ANY] * 3,
-            scratch_shapes=body_scratch(N_SLOTS_A, 2) + [pltpu.VMEM((ROWS, 3072), BF), pltpu.VMEM((ROWS, 128), F32)] + COMM_SCRATCH + [
-                pltpu.VMEM((1, ROWS), jnp.int32), pltpu.VMEM((3, 2, D), BF), vec, vec, pltpu.VMEM((2, 4, 1408), BF), vec, vec, vec, pltpu.VMEM((2, 1408), F32),
-                pltpu.VMEM((2, D), BF), pltpu.VMEM((3, 3072), BF), pltpu.VMEM((3, 3072), BF), pltpu.VMEM((3, D), BF), pltpu.SemaphoreType.DMA((14,)),
-                pltpu.VMEM((2, 3, ROWS, 1408), BF), pltpu.VMEM((2, ROWS, 1408), F32), pltpu.VMEM((2, 8, 176, 176), BF), pltpu.VMEM((2, 8, 176, 176), BF),
-                pltpu.VMEM((2, ROWS, 1408), BF), pltpu.VMEM((ROWS, 128), F32), pltpu.VMEM((ROWS, 1408), BF), pltpu.VMEM((ROWS, 1408), F32), pltpu.VMEM((ROWS, 1408), F32),
-                pltpu.VMEM((ROWS, 1408), BF), pltpu.VMEM((ROWS, 128), jnp.int32), pltpu.SemaphoreType.DMA((2, 4)), pltpu.SemaphoreType.DMA((2, 3))],
+            out_shape=[shape((ROWS, D), BF), branch, state, head_rows, row, row],
+            in_specs=[ANY] * 28, out_specs=[ANY] * 6,
+            scratch_shapes=body_scratch(N_SLOTS_A, 2) + [hidden, table] + COMM_SCRATCH + [
+                pos_row, scale, vec, vec, pltpu.VMEM((2, 4, LOCAL), BF), vec, vec, vec, vec_f, pltpu.VMEM((2, D), BF), mlp_b, mlp_b, out_b, pltpu.VMEM((1, 128), F32), dma((N_SMALL,)),
+                pltpu.VMEM((3, ROWS, LOCAL), BF), wide_f, gates, gates, wide, table, wide, wide_f, wide_f, wide, pltpu.VMEM((ROWS, 128), jnp.int32),
+                heads, table, table, table, table, dma((2, 4)), dma((2, 2)), dma((3,))],
             compiler_params=pltpu.CompilerParams(collective_id=0, has_side_effects=True, vmem_limit_bytes=VMEM_LIMIT),
             name='recurrent_layers',
-        )(tok, x_in, conv_t, lru_state, norm_scale, rec_wx, rec_bx, rec_wy, rec_by, conv_w, conv_b, gate_wa, gate_ba, gate_wi, gate_bi, a_param, rec_wout, rec_bout, mlp_w1, mlp_b1, mlp_w2, mlp_b2, mlp_wd, mlp_bd)
+        )(tok, x_in, conv_t, lru_state, norm_scale, rec_wx, rec_bx, rec_wy, rec_by, conv_w, conv_b, gate_wa, gate_ba, gate_wi, gate_bi, a_param, rec_wout, rec_bout, mlp_w1, mlp_b1, mlp_w2, mlp_b2, mlp_wd, mlp_bd, freq, attn_wq, attn_wk, attn_wv)
         cache = (ROWS * WINDOW, 128)
-        table = pltpu.VMEM((ROWS, 128), F32)
-        part, conv_out, lru_out, k_out, v_out, slot_out = pl.pallas_call(
+        o_rows, conv_out, lru_out, k_out, v_out, slot_out = pl.pallas_call(
             attention_kernel,
-            out_shape=[shape((N_CHUNK, 2, HALF, CHUNK), BF), shape((2, 3, ROWS, 1408), BF), shape((2, ROWS, 1408), F32), shape(cache, BF), shape(cache, BF), shape((ROWS, WINDOW), jnp.int32)],
-            in_specs=[pl.BlockSpec(memory_space=pltpu.SMEM)] + [ANY] * 14, out_specs=[ANY] * 6,
-            scratch_shapes=body_scratch(N_SLOTS_B, 4) + [
-                table, pltpu.VMEM((3, 2, D), BF), pltpu.VMEM((1, ROWS), jnp.int32), pltpu.VMEM((1, 128), F32), table, table, pltpu.VMEM((2, 3, ROWS, 1408), BF), pltpu.VMEM((2, ROWS, 1408), F32), pltpu.VMEM((ROWS, WINDOW), jnp.int32), pltpu.VMEM((ROWS, WINDOW), F32),
-                pltpu.VMEM((ROWS, 128), jnp.int32), pltpu.VMEM((ROWS * HEADS, 128), F32), pltpu.VMEM((ROWS * HEADS, 128), F32), table, table,
-                pltpu.VMEM((ROWS, 1024), BF), pltpu.VMEM((N_CHUNK, 2, HALF, CHUNK), BF), pltpu.SemaphoreType.DMA((5,)), pltpu.SemaphoreType.DMA((3,)), pltpu.SemaphoreType.DMA((N_SLOTS_B, 2))],
+            out_shape=[head_rows, shape((2, 3, ROWS, LOCAL), BF), state, shape(cache, BF), shape(cache, BF), shape((ROWS, WINDOW), jnp.int32)],
+            in_specs=[pl.BlockSpec(memory_space=pltpu.SMEM)] + [ANY] * 10, out_specs=[ANY] * 6,
+            scratch_shapes=body_scratch(N_SLOTS_B, 2)[:2] + [
+                pos_row, pltpu.VMEM((2, 3, ROWS, LOCAL), BF), pltpu.VMEM((2, ROWS, LOCAL), F32), pltpu.VMEM((ROWS, WINDOW), jnp.int32), pltpu.VMEM((ROWS, WINDOW), F32),
+                heads, heads, table, table, dma((5,)), dma((3,)), dma((N_SLOTS_B, 2))],
             compiler_params=pltpu.CompilerParams(vmem_limit_bytes=VMEM_LIMIT),
             name='attention_layer',
-        )(tok_pos, tok, x_mid, norm_scale, jnp.asarray(FREQ), conv_t, xb, lru_mid, k_cache.reshape(cache), v_cache.reshape(cache), slot_pos, attn_wq, attn_wk, attn_wv, attn_wo)
+        )(tok_pos, tok, q_rows, k_row, v_row, conv_t, xb, lru_mid, k_cache.reshape(cache), v_cache.reshape(cache), slot_pos)
         x_out = pl.pallas_call(
             final_kernel,
             out_shape=shape((ROWS, D), BF),
-            in_specs=[ANY] * 10, out_specs=pl.BlockSpec(memory_space=pltpu.VMEM),
-            scratch_shapes=body_scratch(N_SLOTS_C, 1)[:3] + [pltpu.VMEM((ROWS, 3072), BF), pltpu.VMEM((ROWS, 128), F32)] + COMM_SCRATCH + [
-                pltpu.VMEM((3, 2, D), BF), pltpu.VMEM((D,), BF), pltpu.VMEM((3, 3072), BF), pltpu.VMEM((3, 3072), BF), pltpu.VMEM((3, D), BF), pltpu.SemaphoreType.DMA((7,))],
+            in_specs=[ANY] * 11, out_specs=pl.BlockSpec(memory_space=pltpu.VMEM),
+            scratch_shapes=body_scratch(N_SLOTS_C, 2)[:3] + [hidden, table] + COMM_SCRATCH + [scale, pltpu.VMEM((D,), BF), mlp_b, mlp_b, out_b, heads, pltpu.VMEM((ROWS, WINDOW), BF), dma((7,))],
             compiler_params=pltpu.CompilerParams(collective_id=1, has_side_effects=True, vmem_limit_bytes=VMEM_LIMIT),
             name='last_mlp',
-        )(x_mid, part, norm_scale, attn_bo, mlp_w1, mlp_b1, mlp_w2, mlp_b2, mlp_wd, mlp_bd)
+        )(x_mid, o_rows, norm_scale, attn_bo, attn_wo, mlp_w1, mlp_b1, mlp_w2, mlp_b2, mlp_wd, mlp_bd)
         return (x_out, jnp.transpose(conv_out, (0, 2, 1, 3)), lru_out, k_out.reshape(k_cache.shape), v_out.reshape(v_cache.shape), slot_out)
 
     return jax.shard_map(local_step, mesh=mesh, in_specs=in_specs, out_specs=out_specs, check_vma=False)

time: 214 us -> 202 us (0.944)
  Pallas kernels: 211 us -> 199 us
    pallas_call x2, Pallas kernels: 165 us -> 153 us  [the longest x1 105 us: local_step(): pl.pallas_call(recurrent_kernel, out_shape=[shape((ROWS, D), BF), branch,...]
where the time goes in v3:
time: 202 us
  Pallas kernels  199 us (99%)
  local copies, waits for them, and re-layouts  2.29 us (1%)
    pallas_call x1, Pallas kernels, local_step(): pl.pallas_call(recurrent_kernel, out_shape=[shape((ROWS, D), BF), branch,...  105 us
    pallas_call x1, Pallas kernels, local_step(): pl.pallas_call(attention_kernel, out_shape=[head_rows, shape((2, 3, ROWS,...  48.3 us
    pallas_call x1, Pallas kernels, local_step(): pl.pallas_call(final_kernel, out_shape=shape((ROWS, D), BF), in_specs=[AN...  46 us

profile of v3, /device:TPU:0, one launch (start us, length us, event | category | flops | bytes accessed | tf_op | source)
XLA Modules:
  0.0 201.9 jit_solution(11722093844703563250)
XLA Ops:
  0.6 104.6 %recurrent_layers.1 = (bf16[128,4096]{1,0:T(8,128)(2,1)}, bf16[2,128,1408]{2,1,0:T(8,128)(2,1)}, f32[2,128,1408]{2,1,0:T(8,128)}, f32[1024,128]{1,0:T(8,128)}, f32[128,128]{1,0:T(8,128)}, /*index=5*/f32[128,128]{1,0:T(8,128)}) custom-call(s32[1,128]{1,0:T(1,128)} %bitcast.11, bf16[128,4096]{1,0:T(8,128)(2,1)} %x_in.1, bf16[2,3,128,1408]{3,2,1,0:T(8,128)(2,1)} %bitcast.9, ...), custom_call_target="tpu_custom_call" | custom-call | tf_op jit(solution)/shard_map/recurrent_layers/pallas_call | solution.py:625
  105.2 48.3 %attention_layer.1 = (f32[1024,128]{1,0:T(8,128)}, bf16[2,3,128,1408]{3,2,1,0:T(8,128)(2,1)}, f32[2,128,1408]{2,1,0:T(8,128)}, bf16[131072,128]{1,0:T(8,128)(2,1...) custom-call(s32[128]{0:T(128)} %pos_s.1, s32[1,128]{1,0:T(1,128)} %bitcast.12, f32[1024,128]{1,0:T(8,128)} %get-tuple-element.19.q_in, ...), custom_call_target="tpu_custom_call" | custom-call | tf_op jit(solution)/shard_map/attention_layer/pallas_call | solution.py:637
  153.6 46.0 %last_mlp.1 = bf16[128,4096]{1,0:T(8,128)(2,1)} custom-call(bf16[128,4096]{1,0:T(8,128)(2,1)} %get-tuple-element.18.x_in, f32[1024,128]{1,0:T(8,128)} %get-tuple-element.24.o_in, bf16[3,2,4096]{2,1,0:T(2,128)(2,1)} %nscale.3, bf16[4096]{0:T(1024)(128)(2,1)} %bo.1, bf16[1024,4096]{1,0:T(8,128)(2,1)} %wo.1, bf16[3,4096,3072]{2,1,0:T(8,128)(2,1)} %w1.3, ...), custom_call_target="tpu_custom_call" | custom-call | tf_op jit(solution)/shard_map/last_mlp/pallas_call | solution.py:647
  199.6 2.3 %copy.40 = bf16[128,4096]{1,0:T(8,128)(2,1)} copy(bf16[128,4096]{1,0:T(8,128)(2,1)} %last_mlp.1) | data formatting | bytes 2097152

commit v4 on v3

--- a/solution.py
+++ b/solution.py
@@ -147,6 +147,7 @@
         self.copy3(par, N_CHUNK - 1).wait_recv()
         update(self.other, N_CHUNK - 1, f32(self.r3[N_CHUNK - 1]))
 
+    def sent(self, par):
         @pl.loop(0, N_CHUNK)
         def _(k):
             self.copy1(par, k).wait_send()
@@ -181,6 +182,9 @@
         def _(k):
             gain = 1.0 + f32(self.nscale[row // 2, row % 2:row % 2 + 1, cols(k)])
             self.n[:, cols(k)] = (f32(self.x[:, cols(k)]) * scale * gain).astype(BF)
+
+        if self.n_ar:
+            self.comm.sent((self.n_ar - 1) % 2)
 
     def updater(self, bias, row):
         def update(half, k, u):
@@ -264,27 +268,31 @@
             for h in range(2):
                 st.issue(ahead + 2 * p + h, ahead, stop)
 
-        if layer == 0:
-            self.comm.meet()
-        last_x, = dots(x_tiles, [4])
-        g, = dots(mixed, [0])
-        for h in range(2):
-            st.issue(ahead + 4 + h, ahead, stop)
-        put_x(4, last_x)
-        v.xb[:, 1280:1408] = (g[:, 0:128] + f32(v.bx[layer:layer + 1, 1280:1408])).astype(BF)
-        v.yg[...] = gelu(g[:, 128:256] + f32(v.by[layer:layer + 1, 1280:1408]))
-
         outs.wait_inputs(layer)
         pos = v.tokc[...]
 
-        @pl.loop(0, 11)
-        def _(i):
-            c = cols(i, 128)
+        def conv(i):
+            c = slice(128 * i, 128 * (i + 1))
             acc = f32(v.cb[layer:layer + 1, c]) + f32(v.cw[layer, 0:1, c]) * f32(v.xb[:, c])
             for j in range(3):
                 acc = acc + jnp.where(pos >= 3 - j, f32(v.conv[j, :, c]), 0.0) * f32(v.cw[layer, 3 - j:4 - j, c])
             v.xc[:, c] = acc.astype(BF)
 
+        if layer == 0:
+            self.comm.meet()
+        slots = [st.wait(x_tiles, 4), st.wait(mixed, 0)]
+        last_x, g = [jnp.dot(self.n[...], st.slots[slot], preferred_element_type=F32) for slot in slots]
+        for i in range(8):
+            conv(i)
+        put_x(4, last_x)
+        v.xb[:, 1280:] = (g[:, :128] + f32(v.bx[layer:layer + 1, 1280:])).astype(BF)
+        v.yg[...] = gelu(g[:, 128:] + f32(v.by[layer:layer + 1, 1280:]))
+        for h in range(2):
+            st.issue(ahead + 4 + h, ahead, stop)
+
+        first_y, = dots(y_tiles, [0])
+        for i in range(8, 11):
+            conv(i)
         for b in range(8):
             c = slice(176 * b, 176 * (b + 1))
             xc = v.xc[:, c]
@@ -308,16 +316,16 @@
                 y = gelu(g[:, 128 * h:128 * (h + 1)] + f32(v.by[layer:layer + 1, c]))
                 v.gated[:, c] = (new * y).astype(BF)
 
+        put_y(0, first_y)
+        st.issue(ahead + 6, ahead, stop)
+
         @pl.loop(0, 2)
         def _(p):
-            for h, g in enumerate(dots(y_tiles, [2 * p, 2 * p + 1])):
-                put_y(2 * p + h, g)
+            for h, g in enumerate(dots(y_tiles, [2 * p + 1, 2 * p + 2])):
+                put_y(2 * p + 1 + h, g)
             for h in range(2):
-                st.issue(ahead + 6 + 2 * p + h, ahead, stop)
-
-        g, = dots(y_tiles, [4])
-        st.issue(ahead + 10, ahead, stop)
-        put_y(4, g)
+                st.issue(ahead + 7 + 2 * p + h, ahead, stop)
+
         c = slice(1280, 1408)
         v.gated[:, c] = (gate(c, pos == 0) * v.yg[...]).astype(BF)
         outs.write(layer)
@@ -487,14 +495,16 @@
     start(early)
     comm.greet()
     stream.prime(0, N_SLOTS_C)
-    finish(early)
+    early[0].wait()
     for h in range(HEADS):
         o_bf[:, 128 * h:128 * (h + 1)] = o3[pl.ds(h, ROWS, stride=HEADS), :].astype(BF)
     comm.meet()
     body.down(ot, WINDOW, 1, o_bf)
+    finish(early[1:])
     body.all_reduce(v_bo, None)
     body.norm(5)
     body.mlp(up, down, 2, v_b1, v_b2, v_bd)
+    comm.sent(1)
 
 
 GROUP = 4

time: 202 us -> 200 us (0.990)
  no operation moved by 1% of the time
where the time goes in v4:
time: 200 us
  Pallas kernels  197 us (98%)
  local copies, waits for them, and re-layouts  2.29 us (1%)
    pallas_call x1, Pallas kernels, local_step(): pl.pallas_call(recurrent_kernel, out_shape=[shape((ROWS, D), BF), branch,...  103 us
    pallas_call x1, Pallas kernels, local_step(): pl.pallas_call(attention_kernel, out_shape=[head_rows, shape((2, 3, ROWS,...  48.3 us
    pallas_call x1, Pallas kernels, local_step(): pl.pallas_call(final_kernel, out_shape=shape((ROWS, D), BF), in_specs=[AN...  45.8 us

profile of v4, /device:TPU:0, one launch (start us, length us, event | category | flops | bytes accessed | tf_op | source)
XLA Modules:
  0.0 200.0 jit_solution(16850860117207903004)
XLA Ops:
  0.6 102.9 %recurrent_layers.1 = (bf16[128,4096]{1,0:T(8,128)(2,1)}, bf16[2,128,1408]{2,1,0:T(8,128)(2,1)}, f32[2,128,1408]{2,1,0:T(8,128)}, f32[1024,128]{1,0:T(8,128)}, f32[128,128]{1,0:T(8,128)}, /*index=5*/f32[128,128]{1,0:T(8,128)}) custom-call(s32[1,128]{1,0:T(1,128)} %bitcast.11, bf16[128,4096]{1,0:T(8,128)(2,1)} %x_in.1, bf16[2,3,128,1408]{3,2,1,0:T(8,128)(2,1)} %bitcast.9, ...), custom_call_target="tpu_custom_call" | custom-call | tf_op jit(solution)/shard_map/recurrent_layers/pallas_call | solution.py:635
  103.6 48.3 %attention_layer.1 = (f32[1024,128]{1,0:T(8,128)}, bf16[2,3,128,1408]{3,2,1,0:T(8,128)(2,1)}, f32[2,128,1408]{2,1,0:T(8,128)}, bf16[131072,128]{1,0:T(8,128)(2,1...) custom-call(s32[128]{0:T(128)} %pos_s.1, s32[1,128]{1,0:T(1,128)} %bitcast.12, f32[1024,128]{1,0:T(8,128)} %get-tuple-element.19.q_in, ...), custom_call_target="tpu_custom_call" | custom-call | tf_op jit(solution)/shard_map/attention_layer/pallas_call | solution.py:647
  151.9 45.8 %last_mlp.1 = bf16[128,4096]{1,0:T(8,128)(2,1)} custom-call(bf16[128,4096]{1,0:T(8,128)(2,1)} %get-tuple-element.18.x_in, f32[1024,128]{1,0:T(8,128)} %get-tuple-element.24.o_in, bf16[3,2,4096]{2,1,0:T(2,128)(2,1)} %nscale.3, bf16[4096]{0:T(1024)(128)(2,1)} %bo.1, bf16[1024,4096]{1,0:T(8,128)(2,1)} %wo.1, bf16[3,4096,3072]{2,1,0:T(8,128)(2,1)} %w1.3, ...), custom_call_target="tpu_custom_call" | custom-call | tf_op jit(solution)/shard_map/last_mlp/pallas_call | solution.py:657
  197.7 2.3 %copy.40 = bf16[128,4096]{1,0:T(8,128)(2,1)} copy(bf16[128,4096]{1,0:T(8,128)(2,1)} %last_mlp.1) | data formatting | bytes 2097152

commit v5 on v4

--- a/solution.py
+++ b/solution.py
@@ -399,7 +399,7 @@
         c.wait()
 
 
-N_SLOTS_B = 22
+N_SLOTS_B = 25
 N_SLOTS_C = 23
 
 COMM_SCRATCH = [
@@ -509,7 +509,7 @@
 
 GROUP = 4
 N_GROUP = ROWS // GROUP
-LAG = 4
+LAG = 8
 
 
 def attention_kernel(pos_s, tok, q_in, k_row, v_row, conv, xb, lru, k_cache, v_cache, slot_pos, o_out, conv_out, lru_out, k_out, v_out, slot_out,

time: 200 us -> 199 us (level)
  no operation moved by 1% of the time
where the time goes in v5:
time: 199 us
  Pallas kernels  196 us (98%)
  local copies, waits for them, and re-layouts  2.29 us (1%)
    pallas_call x1, Pallas kernels, local_step(): pl.pallas_call(recurrent_kernel, out_shape=[shape((ROWS, D), BF), branch,...  103 us
    pallas_call x1, Pallas kernels, local_step(): pl.pallas_call(attention_kernel, out_shape=[head_rows, shape((2, 3, ROWS,...  47.5 us
    pallas_call x1, Pallas kernels, local_step(): pl.pallas_call(final_kernel, out_shape=shape((ROWS, D), BF), in_specs=[AN...  45.8 us

profile of v5, /device:TPU:0, one launch (start us, length us, event | category | flops | bytes accessed | tf_op | source)
XLA Modules:
  0.0 199.2 jit_solution(11288879042496629625)
XLA Ops:
  0.6 102.9 %recurrent_layers.1 = (bf16[128,4096]{1,0:T(8,128)(2,1)}, bf16[2,128,1408]{2,1,0:T(8,128)(2,1)}, f32[2,128,1408]{2,1,0:T(8,128)}, f32[1024,128]{1,0:T(8,128)}, f32[128,128]{1,0:T(8,128)}, /*index=5*/f32[128,128]{1,0:T(8,128)}) custom-call(s32[1,128]{1,0:T(1,128)} %bitcast.11, bf16[128,4096]{1,0:T(8,128)(2,1)} %x_in.1, bf16[2,3,128,1408]{3,2,1,0:T(8,128)(2,1)} %bitcast.9, ...), custom_call_target="tpu_custom_call" | custom-call | tf_op jit(solution)/shard_map/recurrent_layers/pallas_call | solution.py:635
  103.6 47.5 %attention_layer.1 = (f32[1024,128]{1,0:T(8,128)}, bf16[2,3,128,1408]{3,2,1,0:T(8,128)(2,1)}, f32[2,128,1408]{2,1,0:T(8,128)}, bf16[131072,128]{1,0:T(8,128)(2,1...) custom-call(s32[128]{0:T(128)} %pos_s.1, s32[1,128]{1,0:T(1,128)} %bitcast.12, f32[1024,128]{1,0:T(8,128)} %get-tuple-element.19.q_in, ...), custom_call_target="tpu_custom_call" | custom-call | tf_op jit(solution)/shard_map/attention_layer/pallas_call | solution.py:647
  151.1 45.8 %last_mlp.1 = bf16[128,4096]{1,0:T(8,128)(2,1)} custom-call(bf16[128,4096]{1,0:T(8,128)(2,1)} %get-tuple-element.18.x_in, f32[1024,128]{1,0:T(8,128)} %get-tuple-element.24.o_in, bf16[3,2,4096]{2,1,0:T(2,128)(2,1)} %nscale.3, bf16[4096]{0:T(1024)(128)(2,1)} %bo.1, bf16[1024,4096]{1,0:T(8,128)(2,1)} %wo.1, bf16[3,4096,3072]{2,1,0:T(8,128)(2,1)} %w1.3, ...), custom_call_target="tpu_custom_call" | custom-call | tf_op jit(solution)/shard_map/last_mlp/pallas_call | solution.py:657
  196.9 2.3 %copy.40 = bf16[128,4096]{1,0:T(8,128)(2,1)} copy(bf16[128,4096]{1,0:T(8,128)(2,1)} %last_mlp.1) | data formatting | bytes 2097152
